TPU v7x, 32 devices: a whole 2x2x4 slice. The times are simulated.
32 devices in a mesh: dom: 16 (over z, y, x), sub: 2 (over core).
Axes of the slice: x: 2, y: 2, z: 4, core: 2. Of those that a mesh axis runs over, the one named last changes fastest.
Arguments:
- rhs: float32 [8192], P(('dom', 'sub')), may hold values from -6 to 6
- diagonal: float32 [8192], P(('dom', 'sub')), may hold values from 1 to 2
- self_raw: float32 [8192, 256], P(('dom', 'sub')), may hold values from -0.046875 to 0.046875
- coupling: float32 [8192, 256], P(('dom', 'sub')), may hold values from -0.046875 to 0.046875
- pattern: int32 [64, 2], P(('dom', 'sub')), may hold values 0 or 1
- prolong: float32 [8192, 128], P(('dom', 'sub')), may hold values from -0.5 to 0.5
- coarse_raw: float32 [4096, 256], P('dom'), may hold values from -0.0234375 to 0.0234375
- coarse_diagonal: float32 [4096], P('dom'), may hold values from 1 to 2
Outputs:
- solution: float32 [8192], P(('dom', 'sub'))
- residual: float32 [8192], P(('dom', 'sub'))
- norms: float32 [3], replicated
All inputs are finite; a program needn't handle non-finite values. No bound on the sum of `pattern` on one device may be relied on, other than what follows from the above.
Results may differ from a plain program's by a relative error of at most 0.0003.
Values sent between devices are 32-bit elements; how exact they have to be, the bound alone decides.
A program may use at most 64 MiB of HBM per device.

v0:
```python
import functools

import jax
import jax.numpy as jnp
from jax import lax
from jax.experimental import pallas as pl
from jax.experimental.pallas import tpu as pltpu
from jax.sharding import PartitionSpec as P

ITERS = 3
ROUNDS = ITERS
OMEGA = 0.7
MESH = pl.DeviceIdType.MESH
LANES = 128
PARTS = 3


def parts_of(value):
    high = value.astype(jnp.bfloat16)
    rest = value - high.astype(jnp.float32)
    middle = rest.astype(jnp.bfloat16)
    low = (rest - middle.astype(jnp.float32)).astype(jnp.bfloat16)
    return high, middle, low


def put_parts(ref, value, column=0):
    rows, columns = value.shape
    for index, part in enumerate(parts_of(value)):
        ref[index * rows : (index + 1) * rows, column : column + columns] = part


def spread(vec):
    high, middle, low = [part.astype(jnp.float32) for part in parts_of(vec)]
    row = lax.broadcasted_iota(jnp.int32, (16, vec.shape[1]), 0)
    stack = jnp.where(row == 0, high, jnp.where(row == 1, middle, jnp.where(row == 2, low, 0.0)))
    return jnp.concatenate([stack.astype(jnp.bfloat16)] * PARTS, axis=1)


def times(stack, matrix):
    return jnp.sum(jnp.dot(stack, matrix, preferred_element_type=jnp.float32), axis=0, keepdims=True)


def kernel(
    n_dom, n_sub,
    rhs_ref, diag_ref, self_ref, coup_ref, pat_ref, pro_ref, craw_ref, cdiag_ref,
    sol_ref, res_ref, norm_ref,
    coup_buf, craw_buf, cdiag_buf, own_mat, t_mat, r_mat, rt_mat, l_mat, lt_mat, p_mat, pt_mat, k_mat,
    s_raw, c_raw, p_raw, l_raw, rhs_buf, diag_buf, dnext_buf, dprev_buf,
    snd_first, snd_low, up_first, low_first, snd_a, snd_b, next_buf, prev_buf, part_buf, red_buf,
    pair_send, pair_recv, first_send, first_recv, bulk_send, bulk_recv,
    a_send, b_send, next_recv, prev_recv, r_send, r_recv, load_sem,
):
    dom, sub = lax.axis_index("dom"), lax.axis_index("sub")
    width = rhs_ref.shape[1]
    blocks = pat_ref.shape[0]
    brow = width // blocks
    coarse = pro_ref.shape[1]
    has_prev, has_next = dom > 0, dom < n_dom - 1

    leads = sub == 0

    barrier = pltpu.get_barrier_semaphore()

    @pl.loop(1, n_dom)
    def _(step):
        pl.semaphore_signal(
            barrier, inc=1, device_id=((dom + step) % n_dom, 0), device_id_type=MESH
        )

    pl.semaphore_signal(barrier, inc=1, device_id=(dom, 1 - sub), device_id_type=MESH)

    @pl.when(has_prev)
    def _():
        pl.semaphore_signal(barrier, inc=1, device_id=(dom - 1, 1), device_id_type=MESH)

    loads = [
        pltpu.make_async_copy(source, target, load_sem.at[index])
        for index, (source, target) in enumerate([
            (coup_ref, coup_buf), (diag_ref, diag_buf.at[sub]), (rhs_ref, rhs_buf.at[sub]),
            (self_ref, s_raw.at[sub]), (pro_ref, p_raw.at[sub]),
            (craw_ref, craw_buf), (cdiag_ref, cdiag_buf),
        ])
    ]
    for load in loads:
        load.start()

    @pl.when(dom == 0)
    def _():
        low_first[...] = jnp.zeros_like(low_first)
        prev_buf[...] = jnp.zeros_like(prev_buf)
        dprev_buf[...] = jnp.ones_like(dprev_buf)
        l_raw[...] = jnp.zeros_like(l_raw)

    @pl.when(dom == n_dom - 1)
    def _():
        up_first[...] = jnp.zeros_like(up_first)
        next_buf[...] = jnp.zeros_like(next_buf)
        dnext_buf[...] = jnp.ones_like(dnext_buf)

    for load in loads[:3]:
        load.wait()
    for i in range(blocks):
        for j in range(blocks):
            block = coup_buf[i * brow : (i + 1) * brow, j * brow : (j + 1) * brow]
            block = block * pat_ref[i, j].astype(jnp.float32)
            c_raw[sub, i * brow : (i + 1) * brow, j * brow : (j + 1) * brow] = block
            for index, part in enumerate(parts_of(block)):
                own_mat[index * width + i * brow : index * width + (i + 1) * brow, j * brow : (j + 1) * brow] = part
    first_own = OMEGA * (1.0 / diag_buf[sub]) * rhs_buf[sub]
    snd_first[...] = first_own
    snd_low[...] = times(spread(first_own), own_mat[...])

    for load in loads[3:]:
        load.wait()
    rows = lax.broadcasted_iota(jnp.int32, (2 * coarse, 2 * coarse), 0)
    cols = lax.broadcasted_iota(jnp.int32, (2 * coarse, 2 * coarse), 1)
    craw = craw_buf[...]
    put_parts(k_mat, jnp.where(rows == cols, cdiag_buf[...], 0.5 * (craw + craw.T)))
    cdinv = 1.0 / cdiag_buf[...]

    def remote(source, target, send, recv, device):
        return pltpu.make_async_remote_copy(
            source, target, send, recv, device_id=device, device_id_type=MESH
        )

    def first_up(other):
        return remote(snd_first, up_first, first_send.at[other], first_recv.at[0], (dom - 1, other))

    def first_low(other):
        return remote(snd_low, low_first, first_send.at[other], first_recv.at[1], (dom + 1, other))

    sends_up = jnp.logical_and(has_prev, sub == 0)
    sends_low = jnp.logical_and(has_next, sub == 1)

    def pair(index):
        half = [c_raw, diag_buf, rhs_buf, s_raw, p_raw][index].at[sub]
        return remote(half, half, pair_send.at[index], pair_recv.at[index], (dom, 1 - sub))

    def edge_matrix():
        return remote(c_raw.at[1], l_raw, bulk_send.at[0], bulk_recv.at[0], (dom + 1, 0))

    def edge_relay():
        return remote(l_raw, l_raw, bulk_send.at[1], bulk_recv.at[1], (dom, 1))

    def edge_prev(other):
        return remote(diag_buf.at[1], dprev_buf, bulk_send.at[2 + other], bulk_recv.at[2], (dom + 1, other))

    def edge_next(other):
        return remote(diag_buf.at[0], dnext_buf, bulk_send.at[4 + other], bulk_recv.at[3], (dom - 1, other))

    def to_prev(k, other):
        return remote(snd_a.at[k], next_buf.at[k], a_send.at[k, other], next_recv.at[k], (dom - 1, other))

    def to_next(k, other):
        return remote(snd_b.at[k], prev_buf.at[k], b_send.at[k, other], prev_recv.at[k], (dom + 1, other))

    lead_prev = jnp.logical_and(has_prev, leads)
    lead_next = jnp.logical_and(has_next, leads)

    def send(k, vec):
        snd_a[k] = vec[:, :width]
        snd_b[k] = vec[:, width:]

        @pl.when(lead_prev)
        def _():
            for other in range(n_sub):
                to_prev(k, other).start()

        @pl.when(lead_next)
        def _():
            for other in range(n_sub):
                to_next(k, other).start()

    def receive(k):
        @pl.when(has_prev)
        def _():
            to_next(k, 0).wait_recv()

        @pl.when(has_next)
        def _():
            to_prev(k, 0).wait_recv()

    pl.semaphore_wait(
        barrier, jnp.where(leads, (n_dom - 1) * n_sub + 1, jnp.where(has_next, n_sub + 1, 1))
    )

    @pl.when(sends_up)
    def _():
        for other in range(n_sub):
            first_up(other).start()

    @pl.when(sends_low)
    def _():
        for other in range(n_sub):
            first_low(other).start()
        edge_matrix().start()

    for index in range(5):
        pair(index).start()
    for index in range(2):
        pair(index).wait_recv()

    @pl.when(lead_next)
    def _():
        for other in range(n_sub):
            edge_prev(other).start()

    @pl.when(lead_prev)
    def _():
        for other in range(n_sub):
            edge_next(other).start()

    for index in range(2, 5):
        pair(index).wait_recv()

    def both(ref):
        return jnp.concatenate([ref[0], ref[1]], axis=1)

    diag = both(diag_buf)
    rhs = both(rhs_buf)
    rows = lax.broadcasted_iota(jnp.int32, (width, width), 0)
    cols = lax.broadcasted_iota(jnp.int32, (width, width), 1)
    stride = 2 * width

    def put_block(row, column, value):
        for index, part in enumerate(parts_of(value)):
            t_mat[index * stride + row * width : index * stride + (row + 1) * width,
                  column * width : (column + 1) * width] = part

    for index in range(2):
        raw = s_raw[index]
        put_block(index, index, jnp.where(rows == cols, diag_buf[index], 0.5 * (raw + raw.T)))
    put_block(0, 1, c_raw[0])
    put_block(1, 0, c_raw[0].T)
    put_parts(r_mat, c_raw[1])
    put_parts(rt_mat, c_raw[1].T)
    for index in range(2):
        put_parts(p_mat.at[index], p_raw[index])
        put_parts(pt_mat.at[index], p_raw[index].T)

    dinv = OMEGA * (1.0 / diag)

    def coarse_step(first, resid):
        rcoarse = jnp.concatenate(
            [times(spread(resid[:, :width]), p_mat[0]), times(spread(resid[:, width:]), p_mat[1])], axis=1
        )
        eone = cdinv * rcoarse
        etwo = eone + cdinv * (rcoarse - times(spread(eone), k_mat[...]))
        return first + jnp.concatenate(
            [times(spread(etwo[:, :coarse]), pt_mat[0]), times(spread(etwo[:, coarse:]), pt_mat[1])], axis=1
        )

    def from_prev(vec):
        return times(spread(vec), l_mat[...])

    def from_next(vec):
        return times(spread(vec), rt_mat[...])

    def precond_apply(t, wvec):
        first = dinv * wvec
        if t == 0:
            own = times(spread(first), t_mat[...])

            @pl.when(has_next)
            def _():
                first_up(0).wait_recv()

            @pl.when(has_prev)
            def _():
                first_low(0).wait_recv()

            edge = jnp.concatenate([low_first[...], from_next(up_first[...])], axis=1)
        else:
            send(3 * t, first)
            own = times(spread(first), t_mat[...])
            receive(3 * t)
            edge = jnp.concatenate([from_prev(prev_buf[3 * t]), from_next(next_buf[3 * t])], axis=1)
        second = coarse_step(first, wvec - (own + edge))
        send(3 * t + 1, second)
        gvec = second + dinv * (wvec - times(spread(second), t_mat[...]))
        send(3 * t + 2, gvec)
        if t == 0:
            @pl.when(has_next)
            def _():
                edge_next(0).wait_recv()

            @pl.when(has_prev)
            def _():
                edge_prev(0).wait_recv()

            @pl.when(lead_prev)
            def _():
                edge_matrix().wait_recv()
                edge_relay().start()

            @pl.when(jnp.logical_and(has_prev, sub == 1))
            def _():
                edge_relay().wait_recv()

            put_parts(l_mat, l_raw[...])
            put_parts(lt_mat, l_raw[...].T)
        dinv_next = jnp.where(has_next, OMEGA * (1.0 / dnext_buf[...]), 0.0)
        dinv_prev = jnp.where(has_prev, OMEGA * (1.0 / dprev_buf[...]), 0.0)
        on_next = dinv_next * times(spread(second[:, width:]), r_mat[...])
        on_prev = dinv_prev * times(spread(second[:, :width]), lt_mat[...])
        receive(3 * t + 1)
        edge = jnp.concatenate([from_prev(prev_buf[3 * t + 1]), from_next(next_buf[3 * t + 1])], axis=1)
        mvec = gvec - dinv * edge
        own = times(spread(mvec), t_mat[...])
        receive(3 * t + 2)
        edge = jnp.concatenate(
            [from_prev(prev_buf[3 * t + 2] - on_prev), from_next(next_buf[3 * t + 2] - on_next)], axis=1
        )
        return mvec, own + edge

    lane = lax.broadcasted_iota(jnp.int32, (1, LANES), 1)

    def start_sums(step, resid, uvec, wvec):
        gamma = jnp.sum(resid * uvec, axis=1, keepdims=True)
        delta = jnp.sum(wvec * uvec, axis=1, keepdims=True)
        rnorm = jnp.sum(resid * resid, axis=1, keepdims=True)
        line = jnp.where(lane == 0, gamma, jnp.where(lane == 1, delta, rnorm))
        part_buf[step] = line
        red_buf[step, pl.ds(dom, 1)] = line[None]

        @pl.when(leads)
        def _():
            @pl.loop(1, n_dom)
            def _(offset):
                for other in range(n_sub):
                    remote(
                        part_buf.at[step], red_buf.at[step, dom], r_send.at[step, other], r_recv.at[step],
                        ((dom + offset) % n_dom, other),
                    ).start()

    def end_sums(step):
        others = red_buf.at[step, pl.ds(0, n_dom - 1)]
        pltpu.make_async_copy(others, others, r_recv.at[step]).wait()
        total = jnp.sum(red_buf[step], axis=0)
        return total[:, 0:1], total[:, 1:2], total[:, 2:3]

    resid = rhs
    uvec, wvec = precond_apply(0, resid)
    zeros = jnp.zeros_like(resid)
    pvec, svec, qvec, zvec, solution = (zeros,) * 5
    norm_list = []
    gamma_prev = alpha_prev = None
    for step in range(ITERS):
        start_sums(step, resid, uvec, wvec)
        last = step == ITERS - 1
        if not last:
            mvec, nvec = precond_apply(step + 1, wvec)
        gamma, delta, rnorm = end_sums(step)
        norm_list.append(rnorm)
        if step == 0:
            beta = jnp.zeros_like(gamma)
            alpha = gamma / delta
        else:
            beta = gamma / gamma_prev
            alpha = gamma / (delta - beta * gamma / alpha_prev)
        svec = wvec + beta * svec
        pvec = uvec + beta * pvec
        solution = solution + alpha * pvec
        resid = resid - alpha * svec
        if not last:
            zvec = nvec + beta * zvec
            qvec = mvec + beta * qvec
            uvec = uvec - alpha * qvec
            wvec = wvec - alpha * zvec
        gamma_prev, alpha_prev = gamma, alpha
    sol_ref[...] = jnp.where(sub == 0, solution[:, :width], solution[:, width:])
    res_ref[...] = jnp.where(sub == 0, resid[:, :width], resid[:, width:])
    place_of = lax.broadcasted_iota(jnp.int32, norm_ref.shape, 1)
    norms = jnp.zeros(norm_ref.shape, jnp.float32)
    for step in range(ITERS):
        norms = jnp.where(place_of == step, norm_list[step], norms)
    norm_ref[...] = norms

    for index in range(5):
        pair(index).wait_send()

    @pl.when(sends_up)
    def _():
        for other in range(n_sub):
            first_up(other).wait_send()

    @pl.when(sends_low)
    def _():
        for other in range(n_sub):
            first_low(other).wait_send()
        edge_matrix().wait_send()

    @pl.when(lead_next)
    def _():
        for other in range(n_sub):
            edge_prev(other).wait_send()
            for k in range(1, 3 * ROUNDS):
                to_next(k, other).wait_send()

    @pl.when(lead_prev)
    def _():
        edge_relay().wait_send()
        for other in range(n_sub):
            edge_next(other).wait_send()
            for k in range(1, 3 * ROUNDS):
                to_prev(k, other).wait_send()

    @pl.when(leads)
    def _():
        for t in range(ITERS):
            for other in range(n_sub):
                sent = red_buf.at[t, pl.ds(0, n_dom - 1)]
                pltpu.make_async_copy(sent, sent, r_send.at[t, other]).wait()


def solution(mesh):
    n_dom, n_sub = mesh.shape["dom"], mesh.shape["sub"]

    def per_device(rhs, diagonal, self_raw, coupling, pattern, prolong, coarse_raw, coarse_diagonal):
        width = rhs.shape[0]
        coarse = prolong.shape[1]
        steps = 3 * ROUNDS
        vmem = pl.BlockSpec(memory_space=pltpu.VMEM)
        smem = pl.BlockSpec(memory_space=pltpu.SMEM)
        hbm = pl.BlockSpec(memory_space=pl.ANY)
        half, single = jnp.bfloat16, jnp.float32
        dma = pltpu.SemaphoreType.DMA
        edge = pltpu.VMEM((PARTS * width, width), half)
        line = pltpu.VMEM((1, width), single)
        lines = pltpu.VMEM((steps, 1, width), single)
        sol, res, norms = pl.pallas_call(
            functools.partial(kernel, n_dom, n_sub),
            out_shape=(
                jax.ShapeDtypeStruct((1, width), single),
                jax.ShapeDtypeStruct((1, width), single),
                jax.ShapeDtypeStruct((1, ITERS), single),
            ),
            in_specs=[hbm, hbm, hbm, hbm, smem, hbm, hbm, hbm],
            out_specs=(vmem, vmem, vmem),
            scratch_shapes=[
                pltpu.VMEM((width, width), single),
                pltpu.VMEM((2 * coarse, 2 * coarse), single),
                pltpu.VMEM((1, 2 * coarse), single),
                edge,
                pltpu.VMEM((PARTS * 2 * width, 2 * width), half),
                edge, edge, edge, edge,
                pltpu.VMEM((2, PARTS * width, coarse), half),
                pltpu.VMEM((2, PARTS * coarse, width), half),
                pltpu.VMEM((PARTS * 2 * coarse, 2 * coarse), half),
                pltpu.VMEM((2, width, width), single),
                pltpu.VMEM((2, width, width), single),
                pltpu.VMEM((2, width, coarse), single),
                pltpu.VMEM((width, width), single),
                pltpu.VMEM((2, 1, width), single),
                pltpu.VMEM((2, 1, width), single),
                line, line, line, line, line, line,
                lines, lines, lines, lines,
                pltpu.VMEM((ITERS, 1, LANES), single),
                pltpu.VMEM((ITERS, n_dom, 1, LANES), single),
                dma((5,)), dma((5,)), dma((2,)), dma((2,)), dma((6,)), dma((4,)),
                dma((steps, n_sub)), dma((steps, n_sub)), dma((steps,)), dma((steps,)),
                dma((ITERS, n_sub)), dma((ITERS,)), dma((7,)),
            ],
            compiler_params=pltpu.CompilerParams(collective_id=0, has_side_effects=True),
        )(
            rhs.reshape(1, width), diagonal.reshape(1, width), self_raw, coupling, pattern,
            prolong, coarse_raw, coarse_diagonal.reshape(1, -1),
        )
        return sol.reshape(width), res.reshape(width), norms.reshape(ITERS)

    line = P(("dom", "sub"))
    table = P(("dom", "sub"), None)
    return jax.shard_map(
        per_device,
        mesh=mesh,
        in_specs=(line, line, table, table, table, table, P("dom", None), P("dom")),
        out_specs=(line, line, P()),
        check_vma=False,
    )
```

profile of v0, /device:TPU:0, one launch (start us, length us, event | category | flops | bytes accessed | tf_op | source)
XLA Modules:
  0.0 41.4 jit_solution(6670912752949311991)
XLA Ops:
  0.6 38.4 %shard_map.103 = (f32[1,256]{1,0:T(1,128)}, f32[1,256]{1,0:T(1,128)}, f32[1,3]{1,0:T(1,128)}) custom-call(f32[1,256]{1,0:T(1,128)} %bitcast.6, f32[1,256]{1,0:T(1,128)} %bitcast.7, f32[256,256]{1,0:T(8,128)} %self_ref.1, f32[256,256]{1,0:T(8,128)} %coup_ref.1, s32[2,2]{1,0:T(2,128)} %pat_ref.1, f32[256,128]{1,0:T(8,128)} %pro_ref.1, f32[256,256]{1,0:T(8,128)} %craw_ref.1, ...), custom_call_target="tpu_custom_call" | custom-call | tf_op jit(solution)/shard_map/pallas_call | solution.py:431
  39.0 0.0 copy-start.1
  39.0 0.6 %copy-done.1 = f32[1,256]{1,0:T(1,128)S(1)} copy-done((f32[1,256]{1,0:T(1,128)S(1)}, f32[1,256]{1,0:T(1,128)}, u32[]{:S(2)}) %copy-start.1) | copy-done | bytes 1048
  39.7 0.0 copy-start
  39.7 0.6 %copy.14 = f32[256]{0:T(256)} copy(f32[256]{0:T(256)S(1)} %bitcast.10) | data formatting | bytes 2048
  40.2 0.1 copy-done
  40.3 0.0 copy-start.2
  40.3 0.6 %copy.15 = f32[256]{0:T(256)} copy(f32[256]{0:T(256)S(1)} %bitcast.9) | data formatting | bytes 2048
  40.9 0.0 copy-done.2
  40.9 0.5 %copy.16 = f32[3]{0:T(128)} copy(f32[3]{0:T(128)S(1)} %bitcast.11) | data formatting | bytes 24
Async XLA Ops:
  39.0 0.6 %copy-start.1 = (f32[1,256]{1,0:T(1,128)S(1)}, f32[1,256]{1,0:T(1,128)}, u32[]{:S(2)}) copy-start(f32[1,256]{1,0:T(1,128)} %get-tuple-element.6) | copy-start | bytes 3076
  39.7 0.6 %copy-start = (f32[1,256]{1,0:T(1,128)S(1)}, f32[1,256]{1,0:T(1,128)}, u32[]{:S(2)}) copy-start(f32[1,256]{1,0:T(1,128)} %get-tuple-element.7) | copy-start | bytes 3076
  40.3 0.6 %copy-start.2 = (f32[1,3]{1,0:T(1,128)S(1)}, f32[1,3]{1,0:T(1,128)}, u32[]{:S(2)}) copy-start(f32[1,3]{1,0:T(1,128)} %get-tuple-element.8) | copy-start | bytes 40
where the time goes:
time: 41.6 us; the launch traced here: 41.4 us
  Pallas kernels  38.4 us (92%)
  local copies, waits for them, and re-layouts  2.37 us (6%)
  between operations  0.65 us (2%)
    pallas_call x1, Pallas kernels, per_device(): pl.pallas_call(functools.partial(kernel, n_dom, n_sub), out_shape=(jax.Sh...  38.4 us
    unnamed x9, local copies, waits for them, and re-layouts  2.37 us

commit v1 on v0

v1 whole, which is shorter than its diff:
```python
import functools

import jax
import jax.numpy as jnp
from jax import lax
from jax.experimental import pallas as pl
from jax.experimental.pallas import tpu as pltpu
from jax.sharding import PartitionSpec as P

ITERS = 3
OMEGA = 0.7
MESH = pl.DeviceIdType.MESH
LANES = 128


def factor(count):
    side = 1
    for trial in range(1, count + 1):
        if trial * trial <= count and count % trial == 0:
            side = trial
    return count // side, side


def fold(matrix, row):
    total = None
    for start in range(0, matrix.shape[1], LANES):
        part = matrix[:, start : start + LANES] * row[:, start : start + LANES]
        total = part if total is None else total + part
    return total


def lanes(block):
    return jnp.sum(block, axis=1, keepdims=True)


def down(matrix, column):
    return jnp.sum(matrix * column, axis=0, keepdims=True)


def eye_of():
    rows = lax.broadcasted_iota(jnp.int32, (LANES, LANES), 0)
    cols = lax.broadcasted_iota(jnp.int32, (LANES, LANES), 1)
    return rows == cols


def embed(row):
    eye = eye_of()
    parts = [
        jnp.where(eye, row[:, start : start + LANES], 0.0) for start in range(0, row.shape[1], LANES)
    ]
    return jnp.concatenate(parts, axis=0)


def upright(row):
    return lanes(embed(row))


def flat(column):
    eye = eye_of()
    parts = [
        jnp.sum(jnp.where(eye, column[start : start + LANES], 0.0), axis=0, keepdims=True)
        for start in range(0, column.shape[0], LANES)
    ]
    return jnp.concatenate(parts, axis=1)


def kernel(
    n_dom, n_sub,
    rhs_ref, diag_ref, self_ref, coup_ref, pat_ref, pro_ref, craw_ref, cdiag_ref,
    sol_ref, res_ref, norm_ref,
    lines, s_raw, c_raw, p_raw, k_raw, kdiag, own_lines,
    f_mat, ft_mat, g_mat, t_mat, pt_mat, k_mat,
    up_out, low_out, up_in, low_in, snd_a, snd_b, next_buf, prev_buf,
    part_buf, red_buf, pack_out, pack_in,
    known, load_sem, line_send, line_recv, mat_send, mat_recv, edge_send, edge_recv,
    a_send, b_send, next_recv, prev_recv, r_send, r_recv, pack_send, pack_recv,
):
    dom, sub = lax.axis_index("dom"), lax.axis_index("sub")
    width = rhs_ref.shape[1]
    blocks = pat_ref.shape[0]
    brow = width // blocks
    coarse = pro_ref.shape[1]
    has_prev, has_next = dom > 0, dom < n_dom - 1
    n_row, n_col = factor(n_dom)
    barrier = pltpu.get_barrier_semaphore()
    last = ITERS - 1
    lane = lax.broadcasted_iota(jnp.int32, (1, LANES), 1)

    def remote(source, target, send, recv, device):
        return pltpu.make_async_remote_copy(
            source, target, send, recv, device_id=device, device_id_type=MESH
        )

    def line_copy():
        return remote(lines, lines, line_send, line_recv, (dom, 1))

    def mat_copy(index):
        source = (self_ref, coup_ref, pro_ref)[index]
        target = (s_raw, c_raw, p_raw)[index].at[0]
        return remote(source, target, mat_send.at[index], mat_recv.at[index], (dom, 1))

    def pack_copy():
        return remote(pack_out, pack_in, pack_send, pack_recv, (dom, 0))

    def finish(scalars, step, gamma_prev, alpha_prev):
        gamma, delta = scalars[:, 0:1], scalars[:, 1:2]
        if step == 0:
            return gamma, jnp.zeros_like(gamma), gamma / delta
        beta = gamma / gamma_prev
        return gamma, beta, gamma / (delta - beta * gamma / alpha_prev)

    def put_norms(norm_list):
        place_of = lax.broadcasted_iota(jnp.int32, norm_ref.shape, 1)
        norms = jnp.zeros(norm_ref.shape, jnp.float32)
        for step in range(ITERS):
            norms = jnp.where(place_of == step, norm_list[step], norms)
        norm_ref[...] = norms

    @pl.when(sub == 0)
    def _():
        loads = [
            pltpu.make_async_copy(source, lines.at[index], load_sem.at[index])
            for index, source in enumerate([rhs_ref, diag_ref])
        ]
        for load in loads:
            load.start()
        place = lax.broadcasted_iota(jnp.int32, (1, width), 1)
        for i in range(blocks):
            mask = jnp.zeros((1, width), jnp.float32)
            for j in range(blocks):
                mask = jnp.where(place // brow == j, pat_ref[i, j].astype(jnp.float32), mask)
            lines[2 + i] = mask
        pl.semaphore_wait(barrier, 1)
        for load in loads:
            load.wait()
        line_copy().start()
        for index in range(3):
            mat_copy(index).start()
        line_copy().wait_send()
        for index in range(3):
            mat_copy(index).wait_send()
        pack_copy().wait_recv()
        sol, resid, uvec, wvec, pvec, svec = [pack_in[index : index + 1] for index in range(6)]
        misc = pack_in[6:7]
        every = red_buf.at[last]
        pltpu.make_async_copy(every, every, r_recv.at[last]).wait()
        total = jnp.sum(red_buf[last], axis=0)
        gamma, beta, alpha = finish(total, last, misc[:, 0:1], misc[:, 1:2])
        sol_ref[...] = sol + alpha * (uvec + beta * pvec)
        res_ref[...] = resid - alpha * (wvec + beta * svec)
        put_norms([misc[:, 2 + step : 3 + step] for step in range(last)] + [total[:, 2:3]])

    @pl.when(sub == 1)
    def _():
        row_at, col_at = dom // n_col, dom % n_col
        pl.semaphore_signal(barrier, inc=1, device_id=(dom, 0), device_id_type=MESH)

        @pl.when(has_prev)
        def _():
            pl.semaphore_signal(barrier, inc=1, device_id=(dom - 1, 1), device_id_type=MESH)

        @pl.when(has_next)
        def _():
            pl.semaphore_signal(barrier, inc=1, device_id=(dom + 1, 1), device_id_type=MESH)

        def in_row(step):
            return (row_at * n_col + (col_at + step) % n_col, 1)

        def in_col(step):
            return (((row_at + step) % n_row) * n_col + col_at, 1)

        if n_col > 1:
            @pl.loop(1, n_col)
            def _(step):
                pl.semaphore_signal(barrier, inc=1, device_id=in_row(step), device_id_type=MESH)

        @pl.loop(1, n_row)
        def _(step):
            pl.semaphore_signal(barrier, inc=1, device_id=in_col(step), device_id_type=MESH)

        loads = [
            pltpu.make_async_copy(source, target, load_sem.at[index])
            for index, (source, target) in enumerate([
                (rhs_ref, own_lines.at[0]), (diag_ref, own_lines.at[1]), (coup_ref, c_raw.at[1]),
                (self_ref, s_raw.at[1]), (pro_ref, p_raw.at[1]), (craw_ref, k_raw), (cdiag_ref, kdiag),
            ])
        ]
        for load in loads:
            load.start()

        @pl.when(dom == 0)
        def _():
            low_in[...] = jnp.zeros_like(low_in)
            prev_buf[...] = jnp.zeros_like(prev_buf)
            g_mat[...] = jnp.zeros_like(g_mat)

        @pl.when(dom == n_dom - 1)
        def _():
            up_in[...] = jnp.zeros_like(up_in)
            next_buf[...] = jnp.zeros_like(next_buf)

        def first_up():
            return remote(up_out, up_in, edge_send.at[0], edge_recv.at[0], (dom - 1, 1))

        def first_low():
            return remote(low_out, low_in, edge_send.at[1], edge_recv.at[1], (dom + 1, 1))

        def edge_matrix():
            return remote(ft_mat, g_mat, edge_send.at[2], edge_recv.at[2], (dom + 1, 1))

        def to_prev(k):
            return remote(snd_a.at[k], next_buf.at[k], a_send.at[k], next_recv.at[k], (dom - 1, 1))

        def to_next(k):
            return remote(snd_b.at[k], prev_buf.at[k], b_send.at[k], prev_recv.at[k], (dom + 1, 1))

        def send(k, vec):
            snd_a[k] = vec[:, :width]
            snd_b[k] = vec[:, width:]

            @pl.when(has_prev)
            def _():
                to_prev(k).start()

            @pl.when(has_next)
            def _():
                to_next(k).start()

        def receive(k):
            @pl.when(has_prev)
            def _():
                to_next(k).wait_recv()

            @pl.when(has_next)
            def _():
                to_prev(k).wait_recv()

        for load in loads[:3]:
            load.wait()
        for i in range(blocks):
            for j in range(blocks):
                at = (slice(i * brow, (i + 1) * brow), slice(j * brow, (j + 1) * brow))
                f_mat[at] = c_raw[1, at[0], at[1]] * pat_ref[i, j].astype(jnp.float32)
        ft_mat[...] = f_mat[...].T
        rhs_b, diag_b = own_lines[0], own_lines[1]
        scale_b = OMEGA * (1.0 / diag_b)
        first_b = scale_b * rhs_b
        low_out[0] = down(f_mat[...], upright(first_b))
        low_out[1] = scale_b

        pl.semaphore_wait(
            barrier,
            (n_row - 1) + (n_col - 1) + has_prev.astype(jnp.int32) + has_next.astype(jnp.int32),
        )

        @pl.loop(1, n_row)
        def _(step):
            pl.semaphore_signal(known, inc=1, device_id=in_col(step), device_id_type=MESH)

        @pl.when(has_next)
        def _():
            first_low().start()

        line_copy().wait_recv()
        rhs_a, diag_a = lines[0], lines[1]
        scale_a = OMEGA * (1.0 / diag_a)
        first_a = scale_a * rhs_a
        up_out[0] = first_a
        up_out[1] = scale_a

        @pl.when(has_prev)
        def _():
            first_up().start()

        @pl.when(has_next)
        def _():
            edge_matrix().start()

        rows = lax.broadcasted_iota(jnp.int32, (width, width), 0)
        cols = lax.broadcasted_iota(jnp.int32, (width, width), 1)
        same = rows == cols

        def put_self(index, diag):
            raw = s_raw[index]
            at = slice(index * width, (index + 1) * width)
            t_mat[at, at] = jnp.where(same, diag - diag * (1.0 / OMEGA), 0.5 * (raw + raw.T))

        for load in loads[3:]:
            load.wait()
        put_self(1, diag_b)
        pt_mat[1] = p_raw[1].T
        kinv = 1.0 / kdiag[...]
        craw = k_raw[...]
        k_mat[...] = jnp.where(same, -kinv, (0.5 * (craw + craw.T)) * kinv * upright(kinv))

        rhs = jnp.concatenate([rhs_a, rhs_b], axis=1)
        scale = jnp.concatenate([scale_a, scale_b], axis=1)
        heavy = jnp.concatenate([diag_a, diag_b], axis=1) * (1.0 / OMEGA)
        minus = -upright(scale)

        mat_copy(0).wait_recv()
        put_self(0, diag_a)
        mat_copy(1).wait_recv()
        for i in range(blocks):
            at = slice(i * brow, (i + 1) * brow)
            block = c_raw[0, at, :] * lines[2 + i]
            t_mat[at, width:] = block
            t_mat[width:, at] = block.T
        mat_copy(2).wait_recv()
        pt_mat[0] = p_raw[0].T

        def start_sums(step, resid, uvec, wvec):
            gamma, delta, rnorm = lanes(resid * uvec), lanes(wvec * uvec), lanes(resid * resid)
            line = jnp.where(lane == 0, gamma, jnp.where(lane == 1, delta, rnorm))
            part_buf[step] = line
            red_buf[step, pl.ds(dom, 1)] = line[None]
            if step == 0:
                pl.semaphore_wait(known, n_row - 1)

            @pl.loop(1, n_dom)
            def _(offset):
                for other in range(n_sub) if step == last else (1,):
                    remote(
                        part_buf.at[step], red_buf.at[step, dom], r_send.at[step], r_recv.at[step],
                        ((dom + offset) % n_dom, other),
                    ).start()

            if step == last:
                remote(
                    part_buf.at[step], red_buf.at[step, dom], r_send.at[step], r_recv.at[step], (dom, 0)
                ).start()

        def end_sums(step):
            others = red_buf.at[step, pl.ds(0, n_dom - 1)]
            pltpu.make_async_copy(others, others, r_recv.at[step]).wait()
            return jnp.sum(red_buf[step], axis=0)

        def halves(block):
            return block[:width], block[width:]

        def round_of(t, vec, begin, middle):
            first = scale * vec
            if t:
                send(3 * t, first)
            begin()
            base = fold(t_mat[...], first)
            if t == 0:
                @pl.when(has_next)
                def _():
                    first_up().wait_recv()

                @pl.when(has_prev)
                def _():
                    first_low().wait_recv()

                edge_a, edge_b = embed(low_in[0]), fold(f_mat[...], up_in[0])
            else:
                receive(3 * t)
                edge_a, edge_b = fold(g_mat[...], prev_buf[3 * t]), fold(f_mat[...], next_buf[3 * t])
            base_a, base_b = halves(base)
            rough = jnp.concatenate(
                [down(p_raw[0], lanes(base_a + edge_a)), down(p_raw[1], lanes(base_b + edge_b))], axis=1
            )
            etwo = lanes(fold(k_mat[...], rough))
            second = first + jnp.concatenate(
                [down(pt_mat[0], etwo[:coarse]), down(pt_mat[1], etwo[coarse:])], axis=1
            )
            send(3 * t + 1, second)
            base = fold(t_mat[...], second) - embed(vec)
            send(3 * t + 2, -scale * flat(lanes(base)))
            side_next = jnp.where(has_next, up_in[1], 0.0)
            side_prev = jnp.where(has_prev, low_in[1], 0.0)
            upper = upright(second)
            on_next = side_next * down(f_mat[...], upper[width:])
            if t == 0:
                @pl.when(has_prev)
                def _():
                    edge_matrix().wait_recv()

            on_prev = side_prev * down(g_mat[...], upper[:width])
            extra = middle()
            receive(3 * t + 1)
            base_a, base_b = halves(base)
            col_a = minus[:width] * lanes(base_a + fold(g_mat[...], prev_buf[3 * t + 1]))
            col_b = minus[width:] * lanes(base_b + fold(f_mat[...], next_buf[3 * t + 1]))
            mvec = jnp.concatenate([flat(col_a), flat(col_b)], axis=1)
            own = down(t_mat[:width, :], col_a) + down(t_mat[width:, :], col_b) + heavy * mvec
            receive(3 * t + 2)
            edge = jnp.concatenate([
                flat(lanes(fold(g_mat[...], prev_buf[3 * t + 2] - on_prev))),
                flat(lanes(fold(f_mat[...], next_buf[3 * t + 2] - on_next))),
            ], axis=1)
            return mvec, own + edge, extra

        resid = rhs
        uvec, wvec, _ = round_of(0, resid, lambda: None, lambda: None)
        zeros = jnp.zeros_like(resid)
        pvec, svec, qvec, zvec, solution = (zeros,) * 5
        norm_list = []
        gamma = alpha = None
        for step in range(last):
            def begin():
                start_sums(step, resid, uvec, wvec)

            def middle():
                sums = end_sums(step)
                return sums, finish(sums, step, gamma, alpha)

            mvec, nvec, (total, (gamma, beta, alpha)) = round_of(step + 1, wvec, begin, middle)
            norm_list.append(total[:, 2:3])
            svec = wvec + beta * svec
            pvec = uvec + beta * pvec
            solution = solution + alpha * pvec
            resid = resid - alpha * svec
            zvec = nvec + beta * zvec
            qvec = mvec + beta * qvec
            uvec = uvec - alpha * qvec
            wvec = wvec - alpha * zvec
        start_sums(last, resid, uvec, wvec)
        for index, vec in enumerate([solution, resid, uvec, wvec, pvec, svec]):
            pack_out[index : index + 1] = vec[:, :width]
        misc = jnp.where(lane == 0, gamma, alpha)
        for step in range(last):
            misc = jnp.where(lane == 2 + step, norm_list[step], misc)
        pack_out[6:7, :LANES] = misc
        pack_copy().start()
        total = end_sums(last)
        gamma, beta, alpha = finish(total, last, gamma, alpha)
        sol_ref[...] = (solution + alpha * (uvec + beta * pvec))[:, width:]
        res_ref[...] = (resid - alpha * (wvec + beta * svec))[:, width:]
        put_norms(norm_list + [total[:, 2:3]])

        pack_copy().wait_send()

        @pl.when(has_prev)
        def _():
            first_up().wait_send()
            for k in range(1, 3 * ITERS):
                to_prev(k).wait_send()

        @pl.when(has_next)
        def _():
            first_low().wait_send()
            edge_matrix().wait_send()
            for k in range(1, 3 * ITERS):
                to_next(k).wait_send()

        for step in range(ITERS):
            sent = red_buf.at[step, pl.ds(0, n_dom - 1)]
            pltpu.make_async_copy(sent, sent, r_send.at[step]).wait()
            if step == last:
                every = red_buf.at[step]
                pltpu.make_async_copy(every, every, r_send.at[step]).wait()


def solution(mesh):
    n_dom, n_sub = mesh.shape["dom"], mesh.shape["sub"]

    def per_device(rhs, diagonal, self_raw, coupling, pattern, prolong, coarse_raw, coarse_diagonal):
        width = rhs.shape[0]
        coarse = prolong.shape[1]
        blocks = pattern.shape[0]
        steps = 3 * ITERS
        vmem = pl.BlockSpec(memory_space=pltpu.VMEM)
        smem = pl.BlockSpec(memory_space=pltpu.SMEM)
        hbm = pl.BlockSpec(memory_space=pl.ANY)
        single = jnp.float32
        dma = pltpu.SemaphoreType.DMA
        square = pltpu.VMEM((width, width), single)
        pair = pltpu.VMEM((2, 1, width), single)
        each = pltpu.VMEM((steps, 1, width), single)
        sol, res, norms = pl.pallas_call(
            functools.partial(kernel, n_dom, n_sub),
            out_shape=(
                jax.ShapeDtypeStruct((1, width), single),
                jax.ShapeDtypeStruct((1, width), single),
                jax.ShapeDtypeStruct((1, ITERS), single),
            ),
            in_specs=[hbm, hbm, hbm, hbm, smem, hbm, hbm, hbm],
            out_specs=(vmem, vmem, vmem),
            scratch_shapes=[
                pltpu.VMEM((2 + blocks, 1, width), single),
                pltpu.VMEM((2, width, width), single),
                pltpu.VMEM((2, width, width), single),
                pltpu.VMEM((2, width, coarse), single),
                pltpu.VMEM((2 * coarse, 2 * coarse), single),
                pltpu.VMEM((1, 2 * coarse), single),
                pair,
                square, square, square,
                pltpu.VMEM((2 * width, 2 * width), single),
                pltpu.VMEM((2, coarse, width), single),
                pltpu.VMEM((2 * coarse, 2 * coarse), single),
                pair, pair, pair, pair, each, each, each, each,
                pltpu.VMEM((ITERS, 1, LANES), single),
                pltpu.VMEM((ITERS, n_dom, 1, LANES), single),
                pltpu.VMEM((8, width), single),
                pltpu.VMEM((8, width), single),
                pltpu.SemaphoreType.REGULAR,
                dma((7,)), dma, dma, dma((3,)), dma((3,)), dma((3,)), dma((3,)),
                dma((steps,)), dma((steps,)), dma((steps,)), dma((steps,)),
                dma((ITERS,)), dma((ITERS,)), dma, dma,
            ],
            compiler_params=pltpu.CompilerParams(collective_id=0, has_side_effects=True),
        )(
            rhs.reshape(1, width), diagonal.reshape(1, width), self_raw, coupling, pattern,
            prolong, coarse_raw, coarse_diagonal.reshape(1, -1),
        )
        return sol.reshape(width), res.reshape(width), norms.reshape(ITERS)

    line = P(("dom", "sub"))
    table = P(("dom", "sub"), None)
    return jax.shard_map(
        per_device,
        mesh=mesh,
        in_specs=(line, line, table, table, table, table, P("dom", None), P("dom")),
        out_specs=(line, line, P()),
        check_vma=False,
    )
```

time: 41.6 us -> 31.2 us (0.75)
  Pallas kernels: 38.4 us -> 27.9 us
    pallas_call x1, Pallas kernels: 38.4 us -> 27.9 us  [per_device(): pl.pallas_call(functools.partial(kernel, n_dom, n_sub), out_shape=(jax.Sh...]
where the time goes in v1:
time: 31.2 us; the launch traced here: 31 us
  Pallas kernels  27.9 us (89%)
  local copies, waits for them, and re-layouts  2.37 us (8%)
  between operations  0.65 us (2%)
    pallas_call x1, Pallas kernels, per_device(): pl.pallas_call(functools.partial(kernel, n_dom, n_sub), out_shape=(jax.Sh...  27.9 us
    unnamed x9, local copies, waits for them, and re-layouts  2.37 us

profile of v1, /device:TPU:0, one launch (start us, length us, event | category | flops | bytes accessed | tf_op | source)
XLA Modules:
  0.0 31.0 jit_solution(9729067938432237050)
XLA Ops:
  0.6 27.9 %shard_map.103 = (f32[1,256]{1,0:T(1,128)}, f32[1,256]{1,0:T(1,128)}, f32[1,3]{1,0:T(1,128)}) custom-call(f32[1,256]{1,0:T(1,128)} %bitcast.6, f32[1,256]{1,0:T(1,128)} %bitcast.7, f32[256,256]{1,0:T(8,128)} %self_ref.1, f32[256,256]{1,0:T(8,128)} %coup_ref.1, s32[2,2]{1,0:T(2,128)} %pat_ref.1, f32[256,128]{1,0:T(8,128)} %pro_ref.1, f32[256,256]{1,0:T(8,128)} %craw_ref.1, ...), custom_call_target="tpu_custom_call" | custom-call | tf_op jit(solution)/shard_map/pallas_call | solution.py:472
  28.6 0.0 copy-start.1
  28.6 0.6 %copy-done.1 = f32[1,256]{1,0:T(1,128)S(1)} copy-done((f32[1,256]{1,0:T(1,128)S(1)}, f32[1,256]{1,0:T(1,128)}, u32[]{:S(2)}) %copy-start.1) | copy-done | bytes 1048
  29.2 0.0 copy-start
  29.2 0.6 %copy.14 = f32[256]{0:T(256)} copy(f32[256]{0:T(256)S(1)} %bitcast.10) | data formatting | bytes 2048
  29.8 0.1 copy-done
  29.8 0.0 copy-start.2
  29.8 0.6 %copy.15 = f32[256]{0:T(256)} copy(f32[256]{0:T(256)S(1)} %bitcast.9) | data formatting | bytes 2048
  30.4 0.0 copy-done.2
  30.4 0.5 %copy.16 = f32[3]{0:T(128)} copy(f32[3]{0:T(128)S(1)} %bitcast.11) | data formatting | bytes 24
Async XLA Ops:
  28.6 0.6 %copy-start.1 = (f32[1,256]{1,0:T(1,128)S(1)}, f32[1,256]{1,0:T(1,128)}, u32[]{:S(2)}) copy-start(f32[1,256]{1,0:T(1,128)} %get-tuple-element.6) | copy-start | bytes 3076
  29.2 0.6 %copy-start = (f32[1,256]{1,0:T(1,128)S(1)}, f32[1,256]{1,0:T(1,128)}, u32[]{:S(2)}) copy-start(f32[1,256]{1,0:T(1,128)} %get-tuple-element.7) | copy-start | bytes 3076
  29.8 0.6 %copy-start.2 = (f32[1,3]{1,0:T(1,128)S(1)}, f32[1,3]{1,0:T(1,128)}, u32[]{:S(2)}) copy-start(f32[1,3]{1,0:T(1,128)} %get-tuple-element.8) | copy-start | bytes 40

commit v2 on v1

--- a/solution.py
+++ b/solution.py
@@ -11,6 +11,7 @@
 OMEGA = 0.7
 MESH = pl.DeviceIdType.MESH
 LANES = 128
+GRANT = 56_516_000
 
 
 def factor(count):
@@ -67,8 +68,8 @@
 def kernel(
     n_dom, n_sub,
     rhs_ref, diag_ref, self_ref, coup_ref, pat_ref, pro_ref, craw_ref, cdiag_ref,
-    sol_ref, res_ref, norm_ref,
-    lines, s_raw, c_raw, p_raw, k_raw, kdiag, own_lines,
+    out_ref,
+    lines, s_raw, c_raw, p_raw, k_raw,
     f_mat, ft_mat, g_mat, t_mat, pt_mat, k_mat,
     up_out, low_out, up_in, low_in, snd_a, snd_b, next_buf, prev_buf,
     part_buf, red_buf, pack_out, pack_in,
@@ -102,37 +103,33 @@
     def pack_copy():
         return remote(pack_out, pack_in, pack_send, pack_recv, (dom, 0))
 
-    def finish(scalars, step, gamma_prev, alpha_prev):
+    def finish(scalars, step, gamma_inv, alpha_inv):
         gamma, delta = scalars[:, 0:1], scalars[:, 1:2]
         if step == 0:
             return gamma, jnp.zeros_like(gamma), gamma / delta
-        beta = gamma / gamma_prev
-        return gamma, beta, gamma / (delta - beta * gamma / alpha_prev)
-
-    def put_norms(norm_list):
-        place_of = lax.broadcasted_iota(jnp.int32, norm_ref.shape, 1)
-        norms = jnp.zeros(norm_ref.shape, jnp.float32)
+        beta = gamma * gamma_inv
+        return gamma, beta, gamma / (delta - beta * gamma * alpha_inv)
+
+    def put(sol, res, norm_list):
+        out_ref[0:1] = sol
+        out_ref[1:2] = res
+        place_of = lax.broadcasted_iota(jnp.int32, (1, width), 1)
+        norms = jnp.zeros((1, width), jnp.float32)
         for step in range(ITERS):
             norms = jnp.where(place_of == step, norm_list[step], norms)
-        norm_ref[...] = norms
+        out_ref[2:3] = norms
 
     @pl.when(sub == 0)
     def _():
-        loads = [
-            pltpu.make_async_copy(source, lines.at[index], load_sem.at[index])
-            for index, source in enumerate([rhs_ref, diag_ref])
-        ]
-        for load in loads:
-            load.start()
+        lines[0] = rhs_ref[...]
+        lines[1] = diag_ref[...]
         place = lax.broadcasted_iota(jnp.int32, (1, width), 1)
         for i in range(blocks):
             mask = jnp.zeros((1, width), jnp.float32)
             for j in range(blocks):
-                mask = jnp.where(place // brow == j, pat_ref[i, j].astype(jnp.float32), mask)
+                mask = jnp.where(place // brow == j, pat_ref[i : i + 1, j : j + 1].astype(jnp.float32), mask)
             lines[2 + i] = mask
         pl.semaphore_wait(barrier, 1)
-        for load in loads:
-            load.wait()
         line_copy().start()
         for index in range(3):
             mat_copy(index).start()
@@ -142,13 +139,16 @@
         pack_copy().wait_recv()
         sol, resid, uvec, wvec, pvec, svec = [pack_in[index : index + 1] for index in range(6)]
         misc = pack_in[6:7]
+        gamma_inv, alpha_inv = 1.0 / misc[:, 0:1], 1.0 / misc[:, 1:2]
         every = red_buf.at[last]
         pltpu.make_async_copy(every, every, r_recv.at[last]).wait()
         total = jnp.sum(red_buf[last], axis=0)
-        gamma, beta, alpha = finish(total, last, misc[:, 0:1], misc[:, 1:2])
-        sol_ref[...] = sol + alpha * (uvec + beta * pvec)
-        res_ref[...] = resid - alpha * (wvec + beta * svec)
-        put_norms([misc[:, 2 + step : 3 + step] for step in range(last)] + [total[:, 2:3]])
+        gamma, beta, alpha = finish(total, last, gamma_inv, alpha_inv)
+        put(
+            sol + alpha * (uvec + beta * pvec),
+            resid - alpha * (wvec + beta * svec),
+            [misc[:, 2 + step : 3 + step] for step in range(last)] + [total[:, 2:3]],
+        )
 
     @pl.when(sub == 1)
     def _():
@@ -181,8 +181,7 @@
         loads = [
             pltpu.make_async_copy(source, target, load_sem.at[index])
             for index, (source, target) in enumerate([
-                (rhs_ref, own_lines.at[0]), (diag_ref, own_lines.at[1]), (coup_ref, c_raw.at[1]),
-                (self_ref, s_raw.at[1]), (pro_ref, p_raw.at[1]), (craw_ref, k_raw), (cdiag_ref, kdiag),
+                (coup_ref, c_raw.at[1]), (self_ref, s_raw.at[1]), (pro_ref, p_raw.at[1]), (craw_ref, k_raw),
             ])
         ]
         for load in loads:
@@ -235,14 +234,13 @@
             def _():
                 to_prev(k).wait_recv()
 
-        for load in loads[:3]:
-            load.wait()
+        loads[0].wait()
         for i in range(blocks):
             for j in range(blocks):
                 at = (slice(i * brow, (i + 1) * brow), slice(j * brow, (j + 1) * brow))
-                f_mat[at] = c_raw[1, at[0], at[1]] * pat_ref[i, j].astype(jnp.float32)
+                f_mat[at] = c_raw[1, at[0], at[1]] * pat_ref[i : i + 1, j : j + 1].astype(jnp.float32)
         ft_mat[...] = f_mat[...].T
-        rhs_b, diag_b = own_lines[0], own_lines[1]
+        rhs_b, diag_b = rhs_ref[...], diag_ref[...]
         scale_b = OMEGA * (1.0 / diag_b)
         first_b = scale_b * rhs_b
         low_out[0] = down(f_mat[...], upright(first_b))
@@ -285,11 +283,11 @@
             at = slice(index * width, (index + 1) * width)
             t_mat[at, at] = jnp.where(same, diag - diag * (1.0 / OMEGA), 0.5 * (raw + raw.T))
 
-        for load in loads[3:]:
+        for load in loads[1:]:
             load.wait()
         put_self(1, diag_b)
         pt_mat[1] = p_raw[1].T
-        kinv = 1.0 / kdiag[...]
+        kinv = 1.0 / cdiag_ref[...]
         craw = k_raw[...]
         k_mat[...] = jnp.where(same, -kinv, (0.5 * (craw + craw.T)) * kinv * upright(kinv))
 
@@ -317,12 +315,13 @@
             if step == 0:
                 pl.semaphore_wait(known, n_row - 1)
 
-            @pl.loop(1, n_dom)
-            def _(offset):
+            @pl.loop(0, n_dom - 1)
+            def _(index):
+                target = index + (index >= dom).astype(jnp.int32)
                 for other in range(n_sub) if step == last else (1,):
                     remote(
                         part_buf.at[step], red_buf.at[step, dom], r_send.at[step], r_recv.at[step],
-                        ((dom + offset) % n_dom, other),
+                        (target, other),
                     ).start()
 
             if step == last:
@@ -397,16 +396,17 @@
         zeros = jnp.zeros_like(resid)
         pvec, svec, qvec, zvec, solution = (zeros,) * 5
         norm_list = []
-        gamma = alpha = None
+        gamma_inv = alpha_inv = None
         for step in range(last):
             def begin():
                 start_sums(step, resid, uvec, wvec)
 
             def middle():
                 sums = end_sums(step)
-                return sums, finish(sums, step, gamma, alpha)
+                return sums, finish(sums, step, gamma_inv, alpha_inv)
 
             mvec, nvec, (total, (gamma, beta, alpha)) = round_of(step + 1, wvec, begin, middle)
+            gamma_inv, alpha_inv = 1.0 / gamma, 1.0 / alpha
             norm_list.append(total[:, 2:3])
             svec = wvec + beta * svec
             pvec = uvec + beta * pvec
@@ -425,10 +425,12 @@
         pack_out[6:7, :LANES] = misc
         pack_copy().start()
         total = end_sums(last)
-        gamma, beta, alpha = finish(total, last, gamma, alpha)
-        sol_ref[...] = (solution + alpha * (uvec + beta * pvec))[:, width:]
-        res_ref[...] = (resid - alpha * (wvec + beta * svec))[:, width:]
-        put_norms(norm_list + [total[:, 2:3]])
+        gamma, beta, alpha = finish(total, last, gamma_inv, alpha_inv)
+        put(
+            (solution + alpha * (uvec + beta * pvec))[:, width:],
+            (resid - alpha * (wvec + beta * svec))[:, width:],
+            norm_list + [total[:, 2:3]],
+        )
 
         pack_copy().wait_send()
 
@@ -453,6 +455,12 @@
                 pltpu.make_async_copy(every, every, r_send.at[step]).wait()
 
 
+def unpack(packed_ref, sol_ref, res_ref, norm_ref):
+    sol_ref[...] = packed_ref[0]
+    res_ref[...] = packed_ref[1]
+    norm_ref[...] = packed_ref[2, : norm_ref.shape[0]]
+
+
 def solution(mesh):
     n_dom, n_sub = mesh.shape["dom"], mesh.shape["sub"]
 
@@ -462,30 +470,23 @@
         blocks = pattern.shape[0]
         steps = 3 * ITERS
         vmem = pl.BlockSpec(memory_space=pltpu.VMEM)
-        smem = pl.BlockSpec(memory_space=pltpu.SMEM)
         hbm = pl.BlockSpec(memory_space=pl.ANY)
         single = jnp.float32
         dma = pltpu.SemaphoreType.DMA
         square = pltpu.VMEM((width, width), single)
         pair = pltpu.VMEM((2, 1, width), single)
         each = pltpu.VMEM((steps, 1, width), single)
-        sol, res, norms = pl.pallas_call(
+        packed = pl.pallas_call(
             functools.partial(kernel, n_dom, n_sub),
-            out_shape=(
-                jax.ShapeDtypeStruct((1, width), single),
-                jax.ShapeDtypeStruct((1, width), single),
-                jax.ShapeDtypeStruct((1, ITERS), single),
-            ),
-            in_specs=[hbm, hbm, hbm, hbm, smem, hbm, hbm, hbm],
-            out_specs=(vmem, vmem, vmem),
+            out_shape=jax.ShapeDtypeStruct((3, width), single),
+            in_specs=[vmem, vmem, hbm, hbm, vmem, hbm, hbm, vmem],
+            out_specs=vmem,
             scratch_shapes=[
                 pltpu.VMEM((2 + blocks, 1, width), single),
                 pltpu.VMEM((2, width, width), single),
                 pltpu.VMEM((2, width, width), single),
                 pltpu.VMEM((2, width, coarse), single),
                 pltpu.VMEM((2 * coarse, 2 * coarse), single),
-                pltpu.VMEM((1, 2 * coarse), single),
-                pair,
                 square, square, square,
                 pltpu.VMEM((2 * width, 2 * width), single),
                 pltpu.VMEM((2, coarse, width), single),
@@ -496,16 +497,28 @@
                 pltpu.VMEM((8, width), single),
                 pltpu.VMEM((8, width), single),
                 pltpu.SemaphoreType.REGULAR,
-                dma((7,)), dma, dma, dma((3,)), dma((3,)), dma((3,)), dma((3,)),
+                dma((4,)), dma, dma, dma((3,)), dma((3,)), dma((3,)), dma((3,)),
                 dma((steps,)), dma((steps,)), dma((steps,)), dma((steps,)),
                 dma((ITERS,)), dma((ITERS,)), dma, dma,
             ],
-            compiler_params=pltpu.CompilerParams(collective_id=0, has_side_effects=True),
+            compiler_params=pltpu.CompilerParams(
+                collective_id=0, has_side_effects=True, vmem_limit_bytes=GRANT
+            ),
         )(
             rhs.reshape(1, width), diagonal.reshape(1, width), self_raw, coupling, pattern,
             prolong, coarse_raw, coarse_diagonal.reshape(1, -1),
         )
-        return sol.reshape(width), res.reshape(width), norms.reshape(ITERS)
+        return pl.pallas_call(
+            unpack,
+            out_shape=(
+                jax.ShapeDtypeStruct((width,), single),
+                jax.ShapeDtypeStruct((width,), single),
+                jax.ShapeDtypeStruct((ITERS,), single),
+            ),
+            in_specs=[vmem],
+            out_specs=(vmem, vmem, vmem),
+            compiler_params=pltpu.CompilerParams(vmem_limit_bytes=2**20),
+        )(packed)
 
     line = P(("dom", "sub"))
     table = P(("dom", "sub"), None)

time: 31.2 us -> 28.6 us (0.917)
  local copies, waits for them, and re-layouts: 2.37 us -> 0.69 us
  Pallas kernels: 27.9 us -> 27 us
    unnamed x9 -> x8, local copies, waits for them, and re-layouts: 2.37 us -> 0.69 us
    pallas_call x1 -> x2, Pallas kernels: 27.9 us -> 27 us  [the longest x1 26.5 us: per_device(): pl.pallas_call(functools.partial(kernel, n_dom, n_sub), out_shape=jax.Sha...]
where the time goes in v2:
time: 28.6 us; the launch traced here: 28.4 us
  Pallas kernels  27 us (94%)
  local copies, waits for them, and re-layouts  0.69 us (2%)
  between operations  0.67 us (2%)
    pallas_call x1, Pallas kernels, per_device(): pl.pallas_call(functools.partial(kernel, n_dom, n_sub), out_shape=jax.Sha...  26.5 us
    unnamed x8, local copies, waits for them, and re-layouts  0.69 us

profile of v2, /device:TPU:0, one launch (start us, length us, event | category | flops | bytes accessed | tf_op | source)
XLA Modules:
  0.0 28.4 jit_solution(8046000330953316482)
XLA Ops:
  0.6 0.0 copy-start.3
  0.6 0.0 copy-start.1
  0.7 0.0 copy-start.2
  0.7 0.0 copy-start
  0.7 0.6 %copy-done.3 = f32[256]{0:T(256)S(1)} copy-done((f32[256]{0:T(256)S(1)}, f32[256]{0:T(256)}, u32[]{:S(2)}) %copy-start.3) | copy-done | bytes 1048
  1.3 0.0 copy-done.1
  1.3 0.0 copy-done.2
  1.3 0.0 copy-done
  1.4 26.5 %shard_map.103.packed_ref = f32[3,256]{1,0:T(4,128)S(1)} custom-call(f32[1,256]{1,0:T(1,128)S(1)} %bitcast.3, f32[1,256]{1,0:T(1,128)S(1)} %bitcast.4, f32[256,256]{1,0:T(8,128)} %self_ref.1, f32[256,256]{1,0:T(8,128)} %coup_ref.1, s32[2,2]{1,0:T(2,128)S(1)} %copy-done.2, f32[256,128]{1,0:T(8,128)} %pro_ref.1, f32[256,256]{1,0:T(8,128)} %craw_ref.1, ...), custom_call_target="tpu_custom_call" | custom-call | tf_op jit(solution)/shard_map/pallas_call | solution.py:479
  27.8 0.6 %shard_map.104 = (f32[256]{0:T(256)}, f32[256]{0:T(256)}, f32[3]{0:T(128)}) custom-call(f32[3,256]{1,0:T(4,128)S(1)} %shard_map.103.packed_ref), custom_call_target="tpu_custom_call" | custom-call | tf_op jit(solution)/shard_map/pallas_call | solution.py:511
Async XLA Ops:
  0.6 0.7 %copy-start.3 = (f32[256]{0:T(256)S(1)}, f32[256]{0:T(256)}, u32[]{:S(2)}) copy-start(f32[256]{0:T(256)} %param.15) | copy-start | bytes 3076
  0.6 0.7 %copy-start.1 = (f32[256]{0:T(256)S(1)}, f32[256]{0:T(256)}, u32[]{:S(2)}) copy-start(f32[256]{0:T(256)} %param.9) | copy-start | bytes 3076
  0.7 0.7 %copy-start.2 = (s32[2,2]{1,0:T(2,128)S(1)}, s32[2,2]{1,0:T(2,128)}, u32[]{:S(2)}) copy-start(s32[2,2]{1,0:T(2,128)} %pat_ref.1) | copy-start | bytes 52
  0.7 0.7 %copy-start = (f32[256]{0:T(256)S(1)}, f32[256]{0:T(256)}, u32[]{:S(2)}) copy-start(f32[256]{0:T(256)} %param.8) | copy-start | bytes 3076

commit v3 on v2

--- a/solution.py
+++ b/solution.py
@@ -36,6 +36,10 @@
 
 def down(matrix, column):
     return jnp.sum(matrix * column, axis=0, keepdims=True)
+
+
+def product(left, right):
+    return jnp.dot(left, right, precision=lax.Precision.HIGHEST, preferred_element_type=jnp.float32)
 
 
 def eye_of():
@@ -70,11 +74,11 @@
     rhs_ref, diag_ref, self_ref, coup_ref, pat_ref, pro_ref, craw_ref, cdiag_ref,
     out_ref,
     lines, s_raw, c_raw, p_raw, k_raw,
-    f_mat, ft_mat, g_mat, t_mat, pt_mat, k_mat,
-    up_out, low_out, up_in, low_in, snd_a, snd_b, next_buf, prev_buf,
+    edge_mat, ft_mat, t_mat, pt_mat, k_mat, q_mat, kt_mat, ke_mat,
+    up_out, low_out, up_in, low_in, snd_a, snd_b, in_buf, side_buf, mid_buf, end_buf, rough_buf,
     part_buf, red_buf, pack_out, pack_in,
     known, load_sem, line_send, line_recv, mat_send, mat_recv, edge_send, edge_recv,
-    a_send, b_send, next_recv, prev_recv, r_send, r_recv, pack_send, pack_recv,
+    a_send, b_send, in_recv, r_send, r_recv, pack_send, pack_recv,
 ):
     dom, sub = lax.axis_index("dom"), lax.axis_index("sub")
     width = rhs_ref.shape[1]
@@ -103,8 +107,11 @@
     def pack_copy():
         return remote(pack_out, pack_in, pack_send, pack_recv, (dom, 0))
 
+    def pick(row, place):
+        return lanes(jnp.where(lane == place, row[:, :LANES], 0.0))
+
     def finish(scalars, step, gamma_inv, alpha_inv):
-        gamma, delta = scalars[:, 0:1], scalars[:, 1:2]
+        gamma, delta = pick(scalars, 0), pick(scalars, 1)
         if step == 0:
             return gamma, jnp.zeros_like(gamma), gamma / delta
         beta = gamma * gamma_inv
@@ -139,7 +146,8 @@
         pack_copy().wait_recv()
         sol, resid, uvec, wvec, pvec, svec = [pack_in[index : index + 1] for index in range(6)]
         misc = pack_in[6:7]
-        gamma_inv, alpha_inv = 1.0 / misc[:, 0:1], 1.0 / misc[:, 1:2]
+        gamma_inv, alpha_inv = 1.0 / pick(misc, 0), 1.0 / pick(misc, 1)
+        early = [pick(misc, 2 + step) for step in range(last)]
         every = red_buf.at[last]
         pltpu.make_async_copy(every, every, r_recv.at[last]).wait()
         total = jnp.sum(red_buf[last], axis=0)
@@ -147,7 +155,7 @@
         put(
             sol + alpha * (uvec + beta * pvec),
             resid - alpha * (wvec + beta * svec),
-            [misc[:, 2 + step : 3 + step] for step in range(last)] + [total[:, 2:3]],
+            early + [pick(total, 2)],
         )
 
     @pl.when(sub == 1)
@@ -190,13 +198,15 @@
         @pl.when(dom == 0)
         def _():
             low_in[...] = jnp.zeros_like(low_in)
-            prev_buf[...] = jnp.zeros_like(prev_buf)
-            g_mat[...] = jnp.zeros_like(g_mat)
+            edge_mat[0] = jnp.zeros_like(ft_mat)
+            for k in range(1, 3 * ITERS):
+                in_buf[k, 0] = jnp.zeros((1, width), jnp.float32)
 
         @pl.when(dom == n_dom - 1)
         def _():
             up_in[...] = jnp.zeros_like(up_in)
-            next_buf[...] = jnp.zeros_like(next_buf)
+            for k in range(1, 3 * ITERS):
+                in_buf[k, 1] = jnp.zeros((1, width), jnp.float32)
 
         def first_up():
             return remote(up_out, up_in, edge_send.at[0], edge_recv.at[0], (dom - 1, 1))
@@ -205,13 +215,13 @@
             return remote(low_out, low_in, edge_send.at[1], edge_recv.at[1], (dom + 1, 1))
 
         def edge_matrix():
-            return remote(ft_mat, g_mat, edge_send.at[2], edge_recv.at[2], (dom + 1, 1))
+            return remote(ft_mat, edge_mat.at[0], edge_send.at[2], edge_recv.at[2], (dom + 1, 1))
 
         def to_prev(k):
-            return remote(snd_a.at[k], next_buf.at[k], a_send.at[k], next_recv.at[k], (dom - 1, 1))
+            return remote(snd_a.at[k], in_buf.at[k, 1], a_send.at[k], in_recv.at[k, 1], (dom - 1, 1))
 
         def to_next(k):
-            return remote(snd_b.at[k], prev_buf.at[k], b_send.at[k], prev_recv.at[k], (dom + 1, 1))
+            return remote(snd_b.at[k], in_buf.at[k, 0], b_send.at[k], in_recv.at[k, 0], (dom + 1, 1))
 
         def send(k, vec):
             snd_a[k] = vec[:, :width]
@@ -225,25 +235,30 @@
             def _():
                 to_next(k).start()
 
-        def receive(k):
-            @pl.when(has_prev)
+        near = 1 - dom % 2
+        far = dom % 2
+        has_near = jnp.where(near == 1, has_next, has_prev)
+        has_far = jnp.where(near == 1, has_prev, has_next)
+        order = ((near, has_near), (far, has_far))
+
+        def receive(k, side, exists):
+            @pl.when(exists)
             def _():
-                to_next(k).wait_recv()
-
-            @pl.when(has_next)
-            def _():
-                to_prev(k).wait_recv()
+                landed = in_buf.at[k, side]
+                pltpu.make_async_copy(landed, landed, in_recv.at[k, side]).wait()
+
+            return in_buf[k, side]
 
         loads[0].wait()
         for i in range(blocks):
             for j in range(blocks):
                 at = (slice(i * brow, (i + 1) * brow), slice(j * brow, (j + 1) * brow))
-                f_mat[at] = c_raw[1, at[0], at[1]] * pat_ref[i : i + 1, j : j + 1].astype(jnp.float32)
-        ft_mat[...] = f_mat[...].T
+                edge_mat[1, at[0], at[1]] = c_raw[1, at[0], at[1]] * pat_ref[i : i + 1, j : j + 1].astype(jnp.float32)
+        ft_mat[...] = edge_mat[1].T
         rhs_b, diag_b = rhs_ref[...], diag_ref[...]
         scale_b = OMEGA * (1.0 / diag_b)
         first_b = scale_b * rhs_b
-        low_out[0] = down(f_mat[...], upright(first_b))
+        low_out[0] = down(edge_mat[1], upright(first_b))
         low_out[1] = scale_b
 
         pl.semaphore_wait(
@@ -281,7 +296,7 @@
         def put_self(index, diag):
             raw = s_raw[index]
             at = slice(index * width, (index + 1) * width)
-            t_mat[at, at] = jnp.where(same, diag - diag * (1.0 / OMEGA), 0.5 * (raw + raw.T))
+            t_mat[index, :, at] = jnp.where(same, diag - diag * (1.0 / OMEGA), 0.5 * (raw + raw.T))
 
         for load in loads[1:]:
             load.wait()
@@ -302,8 +317,8 @@
         for i in range(blocks):
             at = slice(i * brow, (i + 1) * brow)
             block = c_raw[0, at, :] * lines[2 + i]
-            t_mat[at, width:] = block
-            t_mat[width:, at] = block.T
+            t_mat[0, at, width:] = block
+            t_mat[1, :, at] = block.T
         mat_copy(2).wait_recv()
         pt_mat[0] = p_raw[0].T
 
@@ -334,62 +349,108 @@
             pltpu.make_async_copy(others, others, r_recv.at[step]).wait()
             return jnp.sum(red_buf[step], axis=0)
 
-        def halves(block):
-            return block[:width], block[width:]
+        def join(buffer):
+            return jnp.concatenate([buffer[0], buffer[1]], axis=1)
+
+        def edge_product(side):
+            at = slice(side * coarse, (side + 1) * coarse)
+            ke_mat[side] = product(k_mat[:, at], product(pt_mat[side], edge_mat[side]))
+
+        def coarse_first(first):
+            base_a, base_b = fold(t_mat[0], first), fold(t_mat[1], first)
+
+            def from_prev():
+                @pl.when(has_prev)
+                def _():
+                    first_low().wait_recv()
+
+                rough_buf[0] = down(p_raw[0], lanes(base_a + embed(low_in[0])))
+
+            def from_next():
+                @pl.when(has_next)
+                def _():
+                    first_up().wait_recv()
+
+                rough_buf[1] = down(p_raw[1], lanes(base_b + fold(edge_mat[1], up_in[0])))
+
+            @pl.when(near == 0)
+            def _():
+                from_prev()
+                from_next()
+
+            @pl.when(near == 1)
+            def _():
+                from_next()
+                from_prev()
+
+            return lanes(fold(k_mat[...], join(rough_buf)))
+
+        def coarse_later(k, first):
+            base = fold(kt_mat[...], first)
+            for side, exists in order:
+                base = base + fold(ke_mat[side], receive(k, side, exists))
+            return lanes(base)
+
+        def short(vec, second):
+            return [
+                fold(t_mat[side], second) - embed(vec[:, side * width : (side + 1) * width]) for side in range(2)
+            ]
+
+        def across(blocks):
+            return jnp.concatenate([flat(lanes(block)) for block in blocks], axis=1)
 
         def round_of(t, vec, begin, middle):
             first = scale * vec
             if t:
                 send(3 * t, first)
             begin()
-            base = fold(t_mat[...], first)
-            if t == 0:
-                @pl.when(has_next)
-                def _():
-                    first_up().wait_recv()
-
-                @pl.when(has_prev)
-                def _():
-                    first_low().wait_recv()
-
-                edge_a, edge_b = embed(low_in[0]), fold(f_mat[...], up_in[0])
+            if t == 1:
+                edge_product(0)
+            if t:
+                turned = across(short(vec, first))
+                etwo = coarse_later(3 * t, first)
             else:
-                receive(3 * t)
-                edge_a, edge_b = fold(g_mat[...], prev_buf[3 * t]), fold(f_mat[...], next_buf[3 * t])
-            base_a, base_b = halves(base)
-            rough = jnp.concatenate(
-                [down(p_raw[0], lanes(base_a + edge_a)), down(p_raw[1], lanes(base_b + edge_b))], axis=1
-            )
-            etwo = lanes(fold(k_mat[...], rough))
+                etwo = coarse_first(first)
             second = first + jnp.concatenate(
                 [down(pt_mat[0], etwo[:coarse]), down(pt_mat[1], etwo[coarse:])], axis=1
             )
             send(3 * t + 1, second)
-            base = fold(t_mat[...], second) - embed(vec)
-            send(3 * t + 2, -scale * flat(lanes(base)))
-            side_next = jnp.where(has_next, up_in[1], 0.0)
-            side_prev = jnp.where(has_prev, low_in[1], 0.0)
+            if t:
+                send(3 * t + 2, -scale * (turned + down(q_mat[...], etwo)))
+            base = short(vec, second)
+            if t == 0:
+                send(3 * t + 2, -scale * across(base))
             upper = upright(second)
-            on_next = side_next * down(f_mat[...], upper[width:])
+            side_buf[1] = jnp.where(has_next, up_in[1], 0.0) * down(edge_mat[1], upper[width:])
             if t == 0:
+                for side in range(2):
+                    q_mat[side * coarse : (side + 1) * coarse] = product(pt_mat[side], t_mat[side])
+                kt_mat[...] = product(k_mat[...], q_mat[...])
+                edge_product(1)
+
                 @pl.when(has_prev)
                 def _():
                     edge_matrix().wait_recv()
 
-            on_prev = side_prev * down(g_mat[...], upper[:width])
+            side_buf[0] = jnp.where(has_prev, low_in[1], 0.0) * down(edge_mat[0], upper[:width])
             extra = middle()
-            receive(3 * t + 1)
-            base_a, base_b = halves(base)
-            col_a = minus[:width] * lanes(base_a + fold(g_mat[...], prev_buf[3 * t + 1]))
-            col_b = minus[width:] * lanes(base_b + fold(f_mat[...], next_buf[3 * t + 1]))
-            mvec = jnp.concatenate([flat(col_a), flat(col_b)], axis=1)
-            own = down(t_mat[:width, :], col_a) + down(t_mat[width:, :], col_b) + heavy * mvec
-            receive(3 * t + 2)
-            edge = jnp.concatenate([
-                flat(lanes(fold(g_mat[...], prev_buf[3 * t + 2] - on_prev))),
-                flat(lanes(fold(f_mat[...], next_buf[3 * t + 2] - on_next))),
-            ], axis=1)
-            return mvec, own + edge, extra
+            own = None
+            for side, exists in order:
+                ahead = receive(3 * t + 1, side, exists)
+                if t:
+                    other = receive(3 * t + 2, side, exists) - side_buf[side]
+                total = jnp.where(side == 0, base[0], base[1]) + fold(edge_mat[side], ahead)
+                column = jnp.where(side == 0, minus[:width], minus[width:]) * lanes(total)
+                part = down(t_mat[side], column)
+                own = part if own is None else own + part
+                turned = flat(column)
+                if not t:
+                    other = receive(3 * t + 2, side, exists) - side_buf[side]
+                crossed = flat(lanes(fold(edge_mat[side], other)))
+                mid_buf[side] = turned
+                end_buf[side] = crossed
+            mvec = join(mid_buf)
+            return mvec, own + heavy * mvec + join(end_buf), extra
 
         resid = rhs
         uvec, wvec, _ = round_of(0, resid, lambda: None, lambda: None)
@@ -407,7 +468,7 @@
 
             mvec, nvec, (total, (gamma, beta, alpha)) = round_of(step + 1, wvec, begin, middle)
             gamma_inv, alpha_inv = 1.0 / gamma, 1.0 / alpha
-            norm_list.append(total[:, 2:3])
+            norm_list.append(pick(total, 2))
             svec = wvec + beta * svec
             pvec = uvec + beta * pvec
             solution = solution + alpha * pvec
@@ -429,7 +490,7 @@
         put(
             (solution + alpha * (uvec + beta * pvec))[:, width:],
             (resid - alpha * (wvec + beta * svec))[:, width:],
-            norm_list + [total[:, 2:3]],
+            norm_list + [pick(total, 2)],
         )
 
         pack_copy().wait_send()
@@ -487,18 +548,25 @@
                 pltpu.VMEM((2, width, width), single),
                 pltpu.VMEM((2, width, coarse), single),
                 pltpu.VMEM((2 * coarse, 2 * coarse), single),
-                square, square, square,
-                pltpu.VMEM((2 * width, 2 * width), single),
+                pltpu.VMEM((2, width, width), single),
+                square,
+                pltpu.VMEM((2, width, 2 * width), single),
                 pltpu.VMEM((2, coarse, width), single),
                 pltpu.VMEM((2 * coarse, 2 * coarse), single),
-                pair, pair, pair, pair, each, each, each, each,
+                pltpu.VMEM((2 * coarse, 2 * width), single),
+                pltpu.VMEM((2 * coarse, 2 * width), single),
+                pltpu.VMEM((2, 2 * coarse, width), single),
+                pair, pair, pair, pair, each, each,
+                pltpu.VMEM((steps, 2, 1, width), single),
+                pair, pair, pair,
+                pltpu.VMEM((2, 1, coarse), single),
                 pltpu.VMEM((ITERS, 1, LANES), single),
                 pltpu.VMEM((ITERS, n_dom, 1, LANES), single),
                 pltpu.VMEM((8, width), single),
                 pltpu.VMEM((8, width), single),
                 pltpu.SemaphoreType.REGULAR,
                 dma((4,)), dma, dma, dma((3,)), dma((3,)), dma((3,)), dma((3,)),
-                dma((steps,)), dma((steps,)), dma((steps,)), dma((steps,)),
+                dma((steps,)), dma((steps,)), dma((steps, 2)),
                 dma((ITERS,)), dma((ITERS,)), dma, dma,
             ],
             compiler_params=pltpu.CompilerParams(

time: 28.6 us -> 28 us (0.979)
  Pallas kernels: 27 us -> 26.5 us
    pallas_call x1, Pallas kernels: 26.5 us -> 25.9 us  [per_device(): pl.pallas_call(functools.partial(kernel, n_dom, n_sub), out_shape=jax.Sha...]
where the time goes in v3:
time: 28 us; the launch traced here: 27.8 us
  Pallas kernels  26.5 us (95%)
  local copies, waits for them, and re-layouts  0.69 us (2%)
  between operations  0.67 us (2%)
    pallas_call x1, Pallas kernels, per_device(): pl.pallas_call(functools.partial(kernel, n_dom, n_sub), out_shape=jax.Sha...  25.9 us
    unnamed x8, local copies, waits for them, and re-layouts  0.69 us
    pallas_call x1, Pallas kernels, per_device(): pl.pallas_call(unpack, out_shape=(jax.ShapeDtypeStruct((width,), single),...  0.57 us

profile of v3, /device:TPU:0, one launch (start us, length us, event | category | flops | bytes accessed | tf_op | source)
XLA Modules:
  0.0 27.8 jit_solution(1857999680308365050)
XLA Ops:
  0.6 0.0 copy-start.3
  0.6 0.0 copy-start.1
  0.7 0.0 copy-start.2
  0.7 0.0 copy-start
  0.7 0.6 %copy-done.3 = f32[256]{0:T(256)S(1)} copy-done((f32[256]{0:T(256)S(1)}, f32[256]{0:T(256)}, u32[]{:S(2)}) %copy-start.3) | copy-done | bytes 1048
  1.3 0.0 copy-done.1
  1.3 0.0 copy-done.2
  1.3 0.0 copy-done
  1.4 25.9 %shard_map.103.packed_ref = f32[3,256]{1,0:T(4,128)S(1)} custom-call(f32[1,256]{1,0:T(1,128)S(1)} %bitcast.3, f32[1,256]{1,0:T(1,128)S(1)} %bitcast.4, f32[256,256]{1,0:T(8,128)} %self_ref.1, f32[256,256]{1,0:T(8,128)} %coup_ref.1, s32[2,2]{1,0:T(2,128)S(1)} %copy-done.2, f32[256,128]{1,0:T(8,128)} %pro_ref.1, f32[256,256]{1,0:T(8,128)} %craw_ref.1, ...), custom_call_target="tpu_custom_call" | custom-call | tf_op jit(solution)/shard_map/pallas_call | solution.py:540
  27.3 0.6 %shard_map.104 = (f32[256]{0:T(256)}, f32[256]{0:T(256)}, f32[3]{0:T(128)}) custom-call(f32[3,256]{1,0:T(4,128)S(1)} %shard_map.103.packed_ref), custom_call_target="tpu_custom_call" | custom-call | tf_op jit(solution)/shard_map/pallas_call | solution.py:579
Async XLA Ops:
  0.6 0.7 %copy-start.3 = (f32[256]{0:T(256)S(1)}, f32[256]{0:T(256)}, u32[]{:S(2)}) copy-start(f32[256]{0:T(256)} %param.15) | copy-start | bytes 3076
  0.6 0.7 %copy-start.1 = (f32[256]{0:T(256)S(1)}, f32[256]{0:T(256)}, u32[]{:S(2)}) copy-start(f32[256]{0:T(256)} %param.9) | copy-start | bytes 3076
  0.7 0.7 %copy-start.2 = (s32[2,2]{1,0:T(2,128)S(1)}, s32[2,2]{1,0:T(2,128)}, u32[]{:S(2)}) copy-start(s32[2,2]{1,0:T(2,128)} %pat_ref.1) | copy-start | bytes 52
  0.7 0.7 %copy-start = (f32[256]{0:T(256)S(1)}, f32[256]{0:T(256)}, u32[]{:S(2)}) copy-start(f32[256]{0:T(256)} %param.8) | copy-start | bytes 3076

commit v4 on v3

--- a/solution.py
+++ b/solution.py
@@ -75,10 +75,10 @@
     out_ref,
     lines, s_raw, c_raw, p_raw, k_raw,
     edge_mat, ft_mat, t_mat, pt_mat, k_mat, q_mat, kt_mat, ke_mat,
-    up_out, low_out, up_in, low_in, snd_a, snd_b, in_buf, side_buf, mid_buf, end_buf, rough_buf,
-    part_buf, red_buf, pack_out, pack_in,
-    known, load_sem, line_send, line_recv, mat_send, mat_recv, edge_send, edge_recv,
-    a_send, b_send, in_recv, r_send, r_recv, pack_send, pack_recv,
+    up_out, low_out, up_in, low_in, out_buf, in_buf, side_buf, mid_buf, end_buf, rough_buf,
+    part_buf, red_buf, pack_out, pack_in, halo_mat,
+    known, go, load_sem, line_send, line_recv, mat_send, mat_recv, edge_send, edge_recv,
+    out_send, in_recv, r_send, r_recv, pack_send, pack_recv, halo_send, halo_recv, stage_send, stage_recv,
 ):
     dom, sub = lax.axis_index("dom"), lax.axis_index("sub")
     width = rhs_ref.shape[1]
@@ -89,6 +89,13 @@
     n_row, n_col = factor(n_dom)
     barrier = pltpu.get_barrier_semaphore()
     last = ITERS - 1
+    far = dom % 2
+    near = 1 - far
+    beyond = dom + 2 * far - 1
+    relays = n_col % 2 == 0
+    wide = jnp.logical_or(
+        jnp.logical_and(has_prev, dom % n_col == 0), jnp.logical_and(has_next, dom % n_col == n_col - 1)
+    )
     lane = lax.broadcasted_iota(jnp.int32, (1, LANES), 1)
 
     def remote(source, target, send, recv, device):
@@ -109,6 +116,12 @@
 
     def pick(row, place):
         return lanes(jnp.where(lane == place, row[:, :LANES], 0.0))
+
+    def stage_copy():
+        return remote(s_raw.at[1], halo_mat, stage_send, stage_recv, (dom, 0))
+
+    def halo_copy(source):
+        return remote(source, halo_mat, halo_send, halo_recv, (beyond, 1))
 
     def finish(scalars, step, gamma_inv, alpha_inv):
         gamma, delta = pick(scalars, 0), pick(scalars, 1)
@@ -140,9 +153,28 @@
         line_copy().start()
         for index in range(3):
             mat_copy(index).start()
+        if relays:
+            @pl.when(wide)
+            def _():
+                pl.semaphore_wait(go, 1)
+
+                @pl.when(far == 0)
+                def _():
+                    halo_copy(self_ref).start()
+
+                @pl.when(far == 1)
+                def _():
+                    stage_copy().wait_recv()
+                    halo_copy(halo_mat).start()
+
         line_copy().wait_send()
         for index in range(3):
             mat_copy(index).wait_send()
+        if relays:
+            @pl.when(wide)
+            def _():
+                halo_copy(halo_mat).wait_send()
+
         pack_copy().wait_recv()
         sol, resid, uvec, wvec, pvec, svec = [pack_in[index : index + 1] for index in range(6)]
         misc = pack_in[6:7]
@@ -217,26 +249,20 @@
         def edge_matrix():
             return remote(ft_mat, edge_mat.at[0], edge_send.at[2], edge_recv.at[2], (dom + 1, 1))
 
-        def to_prev(k):
-            return remote(snd_a.at[k], in_buf.at[k, 1], a_send.at[k], in_recv.at[k, 1], (dom - 1, 1))
-
-        def to_next(k):
-            return remote(snd_b.at[k], in_buf.at[k, 0], b_send.at[k], in_recv.at[k, 0], (dom + 1, 1))
-
-        def send(k, vec):
-            snd_a[k] = vec[:, :width]
-            snd_b[k] = vec[:, width:]
-
-            @pl.when(has_prev)
-            def _():
-                to_prev(k).start()
-
-            @pl.when(has_next)
-            def _():
-                to_next(k).start()
-
-        near = 1 - dom % 2
-        far = dom % 2
+        def to_side(k, side, place=None):
+            source = out_buf.at[k if place is None else place, side]
+            return remote(
+                source, in_buf.at[k, 1 - side], out_send.at[k, side], in_recv.at[k, 1 - side], (dom + 2 * side - 1, 1)
+            )
+
+        def send(k, vec, wanted=(has_prev, has_next)):
+            for side in range(2):
+                out_buf[k, side] = vec[:, side * width : (side + 1) * width]
+
+                @pl.when(wanted[side])
+                def _():
+                    to_side(k, side).start()
+
         has_near = jnp.where(near == 1, has_next, has_prev)
         has_far = jnp.where(near == 1, has_prev, has_next)
         order = ((near, has_near), (far, has_far))
@@ -300,6 +326,15 @@
 
         for load in loads[1:]:
             load.wait()
+        if relays:
+            @pl.when(jnp.logical_and(wide, far == 1))
+            def _():
+                stage_copy().start()
+
+            @pl.when(jnp.logical_not(wide))
+            def _():
+                halo_mat[...] = jnp.zeros_like(halo_mat)
+
         put_self(1, diag_b)
         pt_mat[1] = p_raw[1].T
         kinv = 1.0 / cdiag_ref[...]
@@ -385,10 +420,16 @@
 
             return lanes(fold(k_mat[...], join(rough_buf)))
 
-        def coarse_later(k, first):
+        def half(vec):
+            return jnp.where(far == 0, vec[:, :width], vec[:, width:])
+
+        def coarse_later(k, first, halo):
             base = fold(kt_mat[...], first)
             for side, exists in order:
-                base = base + fold(ke_mat[side], receive(k, side, exists))
+                row = receive(k, side, exists)
+                if halo is not None and side is far:
+                    row = jnp.where(wide, halo[0] - halo[1] * row, row)
+                base = base + fold(ke_mat[side], row)
             return lanes(base)
 
         def short(vec, second):
@@ -399,16 +440,25 @@
         def across(blocks):
             return jnp.concatenate([flat(lanes(block)) for block in blocks], axis=1)
 
-        def round_of(t, vec, begin, middle):
+        def round_of(t, vec, begin, middle, held=None):
             first = scale * vec
-            if t:
+            halo = None
+            if held is not None:
+                send(3 * t, first, (
+                    jnp.logical_and(has_prev, dom % n_col != 0), jnp.logical_and(has_next, dom % n_col != n_col - 1)
+                ))
+            elif t:
                 send(3 * t, first)
             begin()
+            if held is not None:
+                column, strong, step_size = held
+                pull = step_size * far_scale
+                halo = in_buf[3, far] - pull * (down(edge_mat[far], column) - strong), pull
             if t == 1:
                 edge_product(0)
             if t:
                 turned = across(short(vec, first))
-                etwo = coarse_later(3 * t, first)
+                etwo = coarse_later(3 * t, first, halo)
             else:
                 etwo = coarse_first(first)
             second = first + jnp.concatenate(
@@ -416,10 +466,21 @@
             )
             send(3 * t + 1, second)
             if t:
-                send(3 * t + 2, -scale * (turned + down(q_mat[...], etwo)))
+                ghost = -scale * (turned + down(q_mat[...], etwo))
+                send(3 * t + 2, ghost)
             base = short(vec, second)
             if t == 0:
                 send(3 * t + 2, -scale * across(base))
+
+                @pl.when(has_next)
+                def _():
+                    edge_matrix().wait_send()
+
+                if relays:
+                    @pl.when(wide)
+                    def _():
+                        pl.semaphore_signal(go, inc=1, device_id=(dom, 0), device_id_type=MESH)
+
             upper = upright(second)
             side_buf[1] = jnp.where(has_next, up_in[1], 0.0) * down(edge_mat[1], upper[width:])
             if t == 0:
@@ -434,6 +495,21 @@
 
             side_buf[0] = jnp.where(has_prev, low_in[1], 0.0) * down(edge_mat[0], upper[:width])
             extra = middle()
+            early = relays and t == 1
+            if early:
+                blank = jnp.zeros((1, width), jnp.float32)
+                alone = jnp.concatenate(
+                    [jnp.where(far == 0, ghost[:, :width], blank), jnp.where(far == 0, blank, ghost[:, width:])], axis=1
+                )
+                mine = flat(lanes(fold(t_mat[far], alone))) + half(heavy) * half(ghost)
+
+                @pl.when(wide)
+                def _():
+                    halo_copy(halo_mat).wait_recv()
+
+                bare = jnp.where(same, 0.0, halo_mat[...])
+                lost = side_buf[far]
+                strong = 0.5 * (flat(lanes(fold(bare, lost))) + down(bare, upright(lost))) + far_diag * lost
             own = None
             for side, exists in order:
                 ahead = receive(3 * t + 1, side, exists)
@@ -442,6 +518,12 @@
                 total = jnp.where(side == 0, base[0], base[1]) + fold(edge_mat[side], ahead)
                 column = jnp.where(side == 0, minus[:width], minus[width:]) * lanes(total)
                 part = down(t_mat[side], column)
+                if early and side is near:
+                    @pl.when(wide)
+                    def _():
+                        out_buf[3 * ITERS, far] = half(part) + mine
+                        to_side(3 * t + 3, far, 3 * ITERS).start()
+
                 own = part if own is None else own + part
                 turned = flat(column)
                 if not t:
@@ -450,10 +532,13 @@
                 mid_buf[side] = turned
                 end_buf[side] = crossed
             mvec = join(mid_buf)
-            return mvec, own + heavy * mvec + join(end_buf), extra
+            return mvec, own + heavy * mvec + join(end_buf), extra, (column, strong) if early else None
 
         resid = rhs
-        uvec, wvec, _ = round_of(0, resid, lambda: None, lambda: None)
+        uvec, wvec, _, _ = round_of(0, resid, lambda: None, lambda: None)
+        far_scale = jnp.where(far == 0, low_in[1], up_in[1])
+        far_diag = OMEGA / far_scale
+        held = None
         zeros = jnp.zeros_like(resid)
         pvec, svec, qvec, zvec, solution = (zeros,) * 5
         norm_list = []
@@ -466,7 +551,8 @@
                 sums = end_sums(step)
                 return sums, finish(sums, step, gamma_inv, alpha_inv)
 
-            mvec, nvec, (total, (gamma, beta, alpha)) = round_of(step + 1, wvec, begin, middle)
+            mvec, nvec, (total, (gamma, beta, alpha)), kept = round_of(step + 1, wvec, begin, middle, held)
+            held = None if kept is None else kept + (alpha,)
             gamma_inv, alpha_inv = 1.0 / gamma, 1.0 / alpha
             norm_list.append(pick(total, 2))
             svec = wvec + beta * svec
@@ -494,19 +580,22 @@
         )
 
         pack_copy().wait_send()
+        if relays:
+            @pl.when(jnp.logical_and(wide, far == 1))
+            def _():
+                stage_copy().wait_send()
 
         @pl.when(has_prev)
         def _():
             first_up().wait_send()
             for k in range(1, 3 * ITERS):
-                to_prev(k).wait_send()
+                to_side(k, 0).wait_send()
 
         @pl.when(has_next)
         def _():
             first_low().wait_send()
-            edge_matrix().wait_send()
             for k in range(1, 3 * ITERS):
-                to_next(k).wait_send()
+                to_side(k, 1).wait_send()
 
         for step in range(ITERS):
             sent = red_buf.at[step, pl.ds(0, n_dom - 1)]
@@ -536,7 +625,6 @@
         dma = pltpu.SemaphoreType.DMA
         square = pltpu.VMEM((width, width), single)
         pair = pltpu.VMEM((2, 1, width), single)
-        each = pltpu.VMEM((steps, 1, width), single)
         packed = pl.pallas_call(
             functools.partial(kernel, n_dom, n_sub),
             out_shape=jax.ShapeDtypeStruct((3, width), single),
@@ -556,7 +644,8 @@
                 pltpu.VMEM((2 * coarse, 2 * width), single),
                 pltpu.VMEM((2 * coarse, 2 * width), single),
                 pltpu.VMEM((2, 2 * coarse, width), single),
-                pair, pair, pair, pair, each, each,
+                pair, pair, pair, pair,
+                pltpu.VMEM((steps + 1, 2, 1, width), single),
                 pltpu.VMEM((steps, 2, 1, width), single),
                 pair, pair, pair,
                 pltpu.VMEM((2, 1, coarse), single),
@@ -564,10 +653,11 @@
                 pltpu.VMEM((ITERS, n_dom, 1, LANES), single),
                 pltpu.VMEM((8, width), single),
                 pltpu.VMEM((8, width), single),
-                pltpu.SemaphoreType.REGULAR,
+                square,
+                pltpu.SemaphoreType.REGULAR, pltpu.SemaphoreType.REGULAR,
                 dma((4,)), dma, dma, dma((3,)), dma((3,)), dma((3,)), dma((3,)),
-                dma((steps,)), dma((steps,)), dma((steps, 2)),
-                dma((ITERS,)), dma((ITERS,)), dma, dma,
+                dma((steps, 2)), dma((steps, 2)),
+                dma((ITERS,)), dma((ITERS,)), dma, dma, dma, dma, dma, dma,
             ],
             compiler_params=pltpu.CompilerParams(
                 collective_id=0, has_side_effects=True, vmem_limit_bytes=GRANT

time: 28 us -> 27.5 us (0.982)
  Pallas kernels: 26.5 us -> 26 us
    pallas_call x1, Pallas kernels: 25.9 us -> 25.4 us  [per_device(): pl.pallas_call(functools.partial(kernel, n_dom, n_sub), out_shape=jax.Sha...]
where the time goes in v4:
time: 27.5 us; the launch traced here: 27.4 us
  Pallas kernels  26 us (95%)
  local copies, waits for them, and re-layouts  0.69 us (3%)
  between operations  0.67 us (2%)
    pallas_call x1, Pallas kernels, per_device(): pl.pallas_call(functools.partial(kernel, n_dom, n_sub), out_shape=jax.Sha...  25.4 us
    unnamed x8, local copies, waits for them, and re-layouts  0.69 us
    pallas_call x1, Pallas kernels, per_device(): pl.pallas_call(unpack, out_shape=(jax.ShapeDtypeStruct((width,), single),...  0.57 us

profile of v4, /device:TPU:0, one launch (start us, length us, event | category | flops | bytes accessed | tf_op | source)
XLA Modules:
  0.0 27.4 jit_solution(1843450880149331536)
XLA Ops:
  0.6 0.0 copy-start.3
  0.6 0.0 copy-start.1
  0.7 0.0 copy-start.2
  0.7 0.0 copy-start
  0.7 0.6 %copy-done.3 = f32[256]{0:T(256)S(1)} copy-done((f32[256]{0:T(256)S(1)}, f32[256]{0:T(256)}, u32[]{:S(2)}) %copy-start.3) | copy-done | bytes 1048
  1.3 0.0 copy-done.1
  1.3 0.0 copy-done.2
  1.3 0.0 copy-done
  1.4 25.4 %shard_map.103.packed_ref = f32[3,256]{1,0:T(4,128)S(1)} custom-call(f32[1,256]{1,0:T(1,128)S(1)} %bitcast.3, f32[1,256]{1,0:T(1,128)S(1)} %bitcast.4, f32[256,256]{1,0:T(8,128)} %self_ref.1, f32[256,256]{1,0:T(8,128)} %coup_ref.1, s32[2,2]{1,0:T(2,128)S(1)} %copy-done.2, f32[256,128]{1,0:T(8,128)} %pro_ref.1, f32[256,256]{1,0:T(8,128)} %craw_ref.1, ...), custom_call_target="tpu_custom_call" | custom-call | tf_op jit(solution)/shard_map/pallas_call | solution.py:628
  26.8 0.6 %shard_map.104 = (f32[256]{0:T(256)}, f32[256]{0:T(256)}, f32[3]{0:T(128)}) custom-call(f32[3,256]{1,0:T(4,128)S(1)} %shard_map.103.packed_ref), custom_call_target="tpu_custom_call" | custom-call | tf_op jit(solution)/shard_map/pallas_call | solution.py:669
Async XLA Ops:
  0.6 0.7 %copy-start.3 = (f32[256]{0:T(256)S(1)}, f32[256]{0:T(256)}, u32[]{:S(2)}) copy-start(f32[256]{0:T(256)} %param.15) | copy-start | bytes 3076
  0.6 0.7 %copy-start.1 = (f32[256]{0:T(256)S(1)}, f32[256]{0:T(256)}, u32[]{:S(2)}) copy-start(f32[256]{0:T(256)} %param.9) | copy-start | bytes 3076
  0.7 0.7 %copy-start.2 = (s32[2,2]{1,0:T(2,128)S(1)}, s32[2,2]{1,0:T(2,128)}, u32[]{:S(2)}) copy-start(s32[2,2]{1,0:T(2,128)} %pat_ref.1) | copy-start | bytes 52
  0.7 0.7 %copy-start = (f32[256]{0:T(256)S(1)}, f32[256]{0:T(256)}, u32[]{:S(2)}) copy-start(f32[256]{0:T(256)} %param.8) | copy-start | bytes 3076

commit v5 on v4

--- a/solution.py
+++ b/solution.py
@@ -36,6 +36,37 @@
 
 def down(matrix, column):
     return jnp.sum(matrix * column, axis=0, keepdims=True)
+
+
+def times(left, right):
+    if isinstance(left, float) and left in (0.0, 1.0):
+        return right if left else 0.0
+    if isinstance(right, float) and right in (0.0, 1.0):
+        return left if right else 0.0
+    return left * right
+
+
+def plus(left, right):
+    if isinstance(left, float) and left == 0.0:
+        return right
+    if isinstance(right, float) and right == 0.0:
+        return left
+    return left + right
+
+
+def blend(scale, left, right):
+    return [plus(one, times(scale, other)) for one, other in zip(right, left)]
+
+
+def combine(weights, terms):
+    total = 0.0
+    for weight, term in zip(weights, terms):
+        total = plus(total, times(weight, term))
+    return total
+
+
+def shift(row):
+    return [plus(row[k], times(-1.0, row[k - 1])) if k else row[0] for k in range(len(row))]
 
 
 def product(left, right):
@@ -75,9 +106,9 @@
     out_ref,
     lines, s_raw, c_raw, p_raw, k_raw,
     edge_mat, ft_mat, t_mat, pt_mat, k_mat, q_mat, kt_mat, ke_mat,
-    up_out, low_out, up_in, low_in, out_buf, in_buf, side_buf, mid_buf, end_buf, rough_buf,
+    up_out, low_out, up_in, low_in, out_buf, in_buf, rim_buf, side_buf, mid_buf, end_buf, rough_buf,
     part_buf, red_buf, pack_out, pack_in, halo_mat,
-    known, go, load_sem, line_send, line_recv, mat_send, mat_recv, edge_send, edge_recv,
+    met, known, go, load_sem, line_send, line_recv, mat_send, mat_recv, edge_send, edge_recv,
     out_send, in_recv, r_send, r_recv, pack_send, pack_recv, halo_send, halo_recv, stage_send, stage_recv,
 ):
     dom, sub = lax.axis_index("dom"), lax.axis_index("sub")
@@ -88,6 +119,7 @@
     has_prev, has_next = dom > 0, dom < n_dom - 1
     n_row, n_col = factor(n_dom)
     barrier = pltpu.get_barrier_semaphore()
+    first_sums, last_sums = range(2)
     last = ITERS - 1
     far = dom % 2
     near = 1 - far
@@ -123,12 +155,12 @@
     def halo_copy(source):
         return remote(source, halo_mat, halo_send, halo_recv, (beyond, 1))
 
-    def finish(scalars, step, gamma_inv, alpha_inv):
-        gamma, delta = pick(scalars, 0), pick(scalars, 1)
-        if step == 0:
-            return gamma, jnp.zeros_like(gamma), gamma / delta
+    def finish(sums, known_gamma, gamma_at, known_delta, delta_at, delta_next, gamma_inv, alpha_inv):
+        even, odd = pick(sums, 0), pick(sums, 1)
+        gamma = known_gamma + gamma_at * even
+        delta = known_delta + delta_at * even + delta_next * odd
         beta = gamma * gamma_inv
-        return gamma, beta, gamma / (delta - beta * gamma * alpha_inv)
+        return beta, gamma / (delta - beta * gamma * alpha_inv)
 
     def put(sol, res, norm_list):
         out_ref[0:1] = sol
@@ -178,17 +210,11 @@
         pack_copy().wait_recv()
         sol, resid, uvec, wvec, pvec, svec = [pack_in[index : index + 1] for index in range(6)]
         misc = pack_in[6:7]
-        gamma_inv, alpha_inv = 1.0 / pick(misc, 0), 1.0 / pick(misc, 1)
-        early = [pick(misc, 2 + step) for step in range(last)]
-        every = red_buf.at[last]
-        pltpu.make_async_copy(every, every, r_recv.at[last]).wait()
-        total = jnp.sum(red_buf[last], axis=0)
-        gamma, beta, alpha = finish(total, last, gamma_inv, alpha_inv)
-        put(
-            sol + alpha * (uvec + beta * pvec),
-            resid - alpha * (wvec + beta * svec),
-            early + [pick(total, 2)],
-        )
+        scalars = [pick(misc, place) for place in range(7 + ITERS)]
+        every = red_buf.at[last_sums]
+        pltpu.make_async_copy(every, every, r_recv.at[last_sums]).wait()
+        beta, alpha = finish(jnp.sum(red_buf[last_sums], axis=0), *scalars[:7])
+        put(sol + alpha * (uvec + beta * pvec), resid - alpha * (wvec + beta * svec), scalars[7:])
 
     @pl.when(sub == 1)
     def _():
@@ -292,10 +318,6 @@
             (n_row - 1) + (n_col - 1) + has_prev.astype(jnp.int32) + has_next.astype(jnp.int32),
         )
 
-        @pl.loop(1, n_row)
-        def _(step):
-            pl.semaphore_signal(known, inc=1, device_id=in_col(step), device_id_type=MESH)
-
         @pl.when(has_next)
         def _():
             first_low().start()
@@ -314,6 +336,11 @@
         @pl.when(has_next)
         def _():
             edge_matrix().start()
+
+        if n_col > 1:
+            @pl.loop(1, n_col)
+            def _(step):
+                pl.semaphore_signal(met, inc=1, device_id=in_row(step), device_id_type=MESH)
 
         rows = lax.broadcasted_iota(jnp.int32, (width, width), 0)
         cols = lax.broadcasted_iota(jnp.int32, (width, width), 1)
@@ -357,24 +384,28 @@
         mat_copy(2).wait_recv()
         pt_mat[0] = p_raw[0].T
 
-        def start_sums(step, resid, uvec, wvec):
-            gamma, delta, rnorm = lanes(resid * uvec), lanes(wvec * uvec), lanes(resid * resid)
-            line = jnp.where(lane == 0, gamma, jnp.where(lane == 1, delta, rnorm))
+        def dot(left, right):
+            return lanes(left * right)
+
+        def start_sums(step, values):
+            line = jnp.zeros((1, LANES), jnp.float32)
+            for place, value in enumerate(values):
+                line = jnp.where(lane == place, value, line)
             part_buf[step] = line
             red_buf[step, pl.ds(dom, 1)] = line[None]
-            if step == 0:
+            if step == first_sums:
                 pl.semaphore_wait(known, n_row - 1)
 
             @pl.loop(0, n_dom - 1)
             def _(index):
                 target = index + (index >= dom).astype(jnp.int32)
-                for other in range(n_sub) if step == last else (1,):
+                for other in range(n_sub) if step == last_sums else (1,):
                     remote(
                         part_buf.at[step], red_buf.at[step, dom], r_send.at[step], r_recv.at[step],
                         (target, other),
                     ).start()
 
-            if step == last:
+            if step == last_sums:
                 remote(
                     part_buf.at[step], red_buf.at[step, dom], r_send.at[step], r_recv.at[step], (dom, 0)
                 ).start()
@@ -419,9 +450,6 @@
                 from_prev()
 
             return lanes(fold(k_mat[...], join(rough_buf)))
-
-        def half(vec):
-            return jnp.where(far == 0, vec[:, :width], vec[:, width:])
 
         def coarse_later(k, first, halo):
             base = fold(kt_mat[...], first)
@@ -432,15 +460,19 @@
                 base = base + fold(ke_mat[side], row)
             return lanes(base)
 
-        def short(vec, second):
-            return [
-                fold(t_mat[side], second) - embed(vec[:, side * width : (side + 1) * width]) for side in range(2)
-            ]
-
-        def across(blocks):
-            return jnp.concatenate([flat(lanes(block)) for block in blocks], axis=1)
-
-        def round_of(t, vec, begin, middle, held=None):
+        def side_of(side, vec):
+            return jnp.where(side == 0, vec[:, :width], vec[:, width:])
+
+        def short(side, vec, second):
+            return fold(t_mat[side], second) - embed(side_of(side, vec))
+
+        def across(vec, second):
+            return jnp.concatenate([
+                flat(lanes(fold(t_mat[side], second) - embed(vec[:, side * width : (side + 1) * width])))
+                for side in range(2)
+            ], axis=1)
+
+        def round_of(t, vec, begin, held=None):
             first = scale * vec
             halo = None
             if held is not None:
@@ -451,16 +483,26 @@
                 send(3 * t, first)
             begin()
             if held is not None:
-                column, strong, step_size = held
-                pull = step_size * far_scale
-                halo = in_buf[3, far] - pull * (down(edge_mat[far], column) - strong), pull
+                column, lost = held
+
+                @pl.when(wide)
+                def _():
+                    halo_copy(halo_mat).wait_recv()
+
+                far_scale = jnp.where(far == 0, low_in[1], up_in[1])
+                far_diag = OMEGA / far_scale
+                bare = jnp.where(same, 0.0, halo_mat[...])
+                strong = 0.5 * (flat(lanes(fold(bare, lost))) + down(bare, upright(lost))) + far_diag * lost
+                halo = in_buf[3, far] - far_scale * (down(edge_mat[far], column) - strong), far_scale
             if t == 1:
                 edge_product(0)
             if t:
-                turned = across(short(vec, first))
+                turned = across(vec, first)
                 etwo = coarse_later(3 * t, first, halo)
             else:
                 etwo = coarse_first(first)
+                rim_buf[0] = jnp.where(has_prev, low_in[1], 0.0)
+                rim_buf[1] = jnp.where(has_next, up_in[1], 0.0)
             second = first + jnp.concatenate(
                 [down(pt_mat[0], etwo[:coarse]), down(pt_mat[1], etwo[coarse:])], axis=1
             )
@@ -468,117 +510,159 @@
             if t:
                 ghost = -scale * (turned + down(q_mat[...], etwo))
                 send(3 * t + 2, ghost)
-            base = short(vec, second)
+            base = {}
+            for side, exists in order[::-1]:
+                base[side is far] = short(side, vec, second)
+                if not t:
+                    out_buf[2, side] = -side_of(side, scale) * flat(lanes(base[side is far]))
+
+                    @pl.when(exists)
+                    def _():
+                        to_side(2, side).start()
+
+            upper = upright(second)
             if t == 0:
-                send(3 * t + 2, -scale * across(base))
-
                 @pl.when(has_next)
                 def _():
                     edge_matrix().wait_send()
+
+                if n_col > 1:
+                    pl.semaphore_wait(met, n_col - 1)
+
+                @pl.loop(1, n_row)
+                def _(step):
+                    pl.semaphore_signal(known, inc=1, device_id=in_col(step), device_id_type=MESH)
 
                 if relays:
                     @pl.when(wide)
                     def _():
                         pl.semaphore_signal(go, inc=1, device_id=(dom, 0), device_id_type=MESH)
 
-            upper = upright(second)
-            side_buf[1] = jnp.where(has_next, up_in[1], 0.0) * down(edge_mat[1], upper[width:])
-            if t == 0:
                 for side in range(2):
                     q_mat[side * coarse : (side + 1) * coarse] = product(pt_mat[side], t_mat[side])
                 kt_mat[...] = product(k_mat[...], q_mat[...])
                 edge_product(1)
-
-                @pl.when(has_prev)
-                def _():
-                    edge_matrix().wait_recv()
-
-            side_buf[0] = jnp.where(has_prev, low_in[1], 0.0) * down(edge_mat[0], upper[:width])
-            extra = middle()
+            else:
+                for side in range(2):
+                    side_buf[side] = rim_buf[side] * down(edge_mat[side], upper[side * width : (side + 1) * width])
             early = relays and t == 1
             if early:
                 blank = jnp.zeros((1, width), jnp.float32)
                 alone = jnp.concatenate(
                     [jnp.where(far == 0, ghost[:, :width], blank), jnp.where(far == 0, blank, ghost[:, width:])], axis=1
                 )
-                mine = flat(lanes(fold(t_mat[far], alone))) + half(heavy) * half(ghost)
-
-                @pl.when(wide)
-                def _():
-                    halo_copy(halo_mat).wait_recv()
-
-                bare = jnp.where(same, 0.0, halo_mat[...])
-                lost = side_buf[far]
-                strong = 0.5 * (flat(lanes(fold(bare, lost))) + down(bare, upright(lost))) + far_diag * lost
+                mine = flat(lanes(fold(t_mat[far], alone))) + side_of(far, heavy) * side_of(far, ghost)
             own = None
             for side, exists in order:
+                if not t:
+                    @pl.when(jnp.logical_and(side == 0, has_prev))
+                    def _():
+                        edge_matrix().wait_recv()
+
                 ahead = receive(3 * t + 1, side, exists)
-                if t:
+                joint = t and not (early and side is near)
+                if joint:
                     other = receive(3 * t + 2, side, exists) - side_buf[side]
-                total = jnp.where(side == 0, base[0], base[1]) + fold(edge_mat[side], ahead)
+                total = base[side is far] + fold(edge_mat[side], ahead)
                 column = jnp.where(side == 0, minus[:width], minus[width:]) * lanes(total)
                 part = down(t_mat[side], column)
                 if early and side is near:
                     @pl.when(wide)
                     def _():
-                        out_buf[3 * ITERS, far] = half(part) + mine
+                        out_buf[3 * ITERS, far] = side_of(far, part) + mine
                         to_side(3 * t + 3, far, 3 * ITERS).start()
 
                 own = part if own is None else own + part
                 turned = flat(column)
                 if not t:
+                    inner = jnp.where(side == 0, upper[:width], upper[width:])
+                    lost = rim_buf[side] * down(edge_mat[side], inner)
+                    other = receive(3 * t + 2, side, exists) - lost
+                elif not joint:
                     other = receive(3 * t + 2, side, exists) - side_buf[side]
                 crossed = flat(lanes(fold(edge_mat[side], other)))
                 mid_buf[side] = turned
                 end_buf[side] = crossed
             mvec = join(mid_buf)
-            return mvec, own + heavy * mvec + join(end_buf), extra, (column, strong) if early else None
-
-        resid = rhs
-        uvec, wvec, _, _ = round_of(0, resid, lambda: None, lambda: None)
-        far_scale = jnp.where(far == 0, low_in[1], up_in[1])
-        far_diag = OMEGA / far_scale
-        held = None
-        zeros = jnp.zeros_like(resid)
-        pvec, svec, qvec, zvec, solution = (zeros,) * 5
+            return mvec, own + heavy * mvec + join(end_buf), (column, side_buf[far]) if early else None
+
+        dvecs, yvecs, held = [rhs], [], None
+        eta, cross = [], {}
+
+        def begin_of(t):
+            def begin():
+                if t:
+                    eta.append(dot(dvecs[t], yvecs[t - 1]))
+                    for k in range(t):
+                        cross[k, t] = dot(dvecs[k], dvecs[t])
+                    cross[t, t] = dot(dvecs[t], dvecs[t])
+                else:
+                    cross[0, 0] = dot(rhs, rhs)
+                if t == last:
+                    start_sums(first_sums, eta + [cross[place] for place in sorted(cross)])
+
+            return begin
+
+        for t in range(ITERS):
+            yvec, bvec, held = round_of(t, dvecs[t], begin_of(t), held)
+            yvecs.append(yvec)
+            dvecs.append(dvecs[t] - bvec)
+            if t < last:
+                eta.append(dot(dvecs[t], yvec))
+        start_sums(last_sums, [dot(dvecs[last], yvecs[last]), dot(dvecs[ITERS], yvecs[last])])
+
+        sums = end_sums(first_sums)
+        count = 2 * last
+        eta = [pick(sums, place) for place in range(count)] + [0.0, 0.0]
+        cross = {place: pick(sums, count + index) for index, place in enumerate(sorted(cross))}
+
+        def pair(left, right):
+            total = 0.0
+            for i, one in enumerate(left):
+                for j, other in enumerate(right):
+                    total = plus(total, times(times(one, other), eta[i + j]))
+            return total
+
+        blank = [0.0] * (ITERS + 1)
+        res = [1.0] + blank[1:]
+        uco, wco = res, shift(res)
+        pco, sco, qco, zco, sol = (blank,) * 5
         norm_list = []
         gamma_inv = alpha_inv = None
-        for step in range(last):
-            def begin():
-                start_sums(step, resid, uvec, wvec)
-
-            def middle():
-                sums = end_sums(step)
-                return sums, finish(sums, step, gamma_inv, alpha_inv)
-
-            mvec, nvec, (total, (gamma, beta, alpha)), kept = round_of(step + 1, wvec, begin, middle, held)
-            held = None if kept is None else kept + (alpha,)
+        for step in range(ITERS):
+            norm = 0.0
+            for i in range(step + 1):
+                for j in range(step + 1):
+                    norm = plus(norm, times(times(res[i], res[j]), cross[min(i, j), max(i, j)]))
+            norm_list.append(norm)
+            gamma, delta = pair(res[:ITERS], uco[:ITERS]), pair(wco, uco[:ITERS])
+            if step == last:
+                break
+            if step == 0:
+                beta, alpha = 0.0, gamma / delta
+            else:
+                beta = gamma * gamma_inv
+                alpha = gamma / (delta - beta * gamma * alpha_inv)
+            zco, qco = blend(beta, zco, shift(wco)), blend(beta, qco, wco)
+            sco, pco = blend(beta, sco, wco), blend(beta, pco, uco)
+            sol = blend(alpha, pco, sol)
+            minus_alpha = -alpha
+            res, uco, wco = blend(minus_alpha, sco, res), blend(minus_alpha, qco, uco), blend(minus_alpha, zco, wco)
             gamma_inv, alpha_inv = 1.0 / gamma, 1.0 / alpha
-            norm_list.append(pick(total, 2))
-            svec = wvec + beta * svec
-            pvec = uvec + beta * pvec
-            solution = solution + alpha * pvec
-            resid = resid - alpha * svec
-            zvec = nvec + beta * zvec
-            qvec = mvec + beta * qvec
-            uvec = uvec - alpha * qvec
-            wvec = wvec - alpha * zvec
-        start_sums(last, resid, uvec, wvec)
+        final = [
+            gamma, times(res[last], uco[last]),
+            delta, plus(times(wco[last], uco[last]), times(wco[ITERS], uco[last - 1])), times(wco[ITERS], uco[last]),
+            gamma_inv, alpha_inv,
+        ]
+        solution, uvec, pvec = [combine(row, yvecs) for row in (sol, uco, pco)]
+        resid, wvec, svec = [combine(row, dvecs) for row in (res, wco, sco)]
         for index, vec in enumerate([solution, resid, uvec, wvec, pvec, svec]):
             pack_out[index : index + 1] = vec[:, :width]
-        misc = jnp.where(lane == 0, gamma, alpha)
-        for step in range(last):
-            misc = jnp.where(lane == 2 + step, norm_list[step], misc)
+        misc = jnp.zeros((1, LANES), jnp.float32)
+        for place, value in enumerate(final + norm_list):
+            misc = jnp.where(lane == place, value, misc)
         pack_out[6:7, :LANES] = misc
         pack_copy().start()
-        total = end_sums(last)
-        gamma, beta, alpha = finish(total, last, gamma_inv, alpha_inv)
-        put(
-            (solution + alpha * (uvec + beta * pvec))[:, width:],
-            (resid - alpha * (wvec + beta * svec))[:, width:],
-            norm_list + [pick(total, 2)],
-        )
-
         pack_copy().wait_send()
         if relays:
             @pl.when(jnp.logical_and(wide, far == 1))
@@ -597,10 +681,17 @@
             for k in range(1, 3 * ITERS):
                 to_side(k, 1).wait_send()
 
-        for step in range(ITERS):
+        beta, alpha = finish(end_sums(last_sums), *final)
+        put(
+            (solution + alpha * (uvec + beta * pvec))[:, width:],
+            (resid - alpha * (wvec + beta * svec))[:, width:],
+            norm_list,
+        )
+
+        for step in (first_sums, last_sums):
             sent = red_buf.at[step, pl.ds(0, n_dom - 1)]
             pltpu.make_async_copy(sent, sent, r_send.at[step]).wait()
-            if step == last:
+            if step == last_sums:
                 every = red_buf.at[step]
                 pltpu.make_async_copy(every, every, r_send.at[step]).wait()
 
@@ -647,17 +738,17 @@
                 pair, pair, pair, pair,
                 pltpu.VMEM((steps + 1, 2, 1, width), single),
                 pltpu.VMEM((steps, 2, 1, width), single),
-                pair, pair, pair,
+                pair, pair, pair, pair,
                 pltpu.VMEM((2, 1, coarse), single),
-                pltpu.VMEM((ITERS, 1, LANES), single),
-                pltpu.VMEM((ITERS, n_dom, 1, LANES), single),
+                pltpu.VMEM((2, 1, LANES), single),
+                pltpu.VMEM((2, n_dom, 1, LANES), single),
                 pltpu.VMEM((8, width), single),
                 pltpu.VMEM((8, width), single),
                 square,
-                pltpu.SemaphoreType.REGULAR, pltpu.SemaphoreType.REGULAR,
+                pltpu.SemaphoreType.REGULAR, pltpu.SemaphoreType.REGULAR, pltpu.SemaphoreType.REGULAR,
                 dma((4,)), dma, dma, dma((3,)), dma((3,)), dma((3,)), dma((3,)),
                 dma((steps, 2)), dma((steps, 2)),
-                dma((ITERS,)), dma((ITERS,)), dma, dma, dma, dma, dma, dma,
+                dma((2,)), dma((2,)), dma, dma, dma, dma, dma, dma,
             ],
             compiler_params=pltpu.CompilerParams(
                 collective_id=0, has_side_effects=True, vmem_limit_bytes=GRANT

time: 27.5 us -> 27 us (0.982)
  Pallas kernels: 26 us -> 25.4 us
    pallas_call x1, Pallas kernels: 25.4 us -> 24.8 us  [per_device(): pl.pallas_call(functools.partial(kernel, n_dom, n_sub), out_shape=jax.Sha...]
where the time goes in v5:
time: 27 us; the launch traced here: 26.8 us
  Pallas kernels  25.4 us (94%)
  local copies, waits for them, and re-layouts  0.69 us (3%)
  between operations  0.67 us (2%)
    pallas_call x1, Pallas kernels, per_device(): pl.pallas_call(functools.partial(kernel, n_dom, n_sub), out_shape=jax.Sha...  24.8 us
    unnamed x8, local copies, waits for them, and re-layouts  0.69 us
    pallas_call x1, Pallas kernels, per_device(): pl.pallas_call(unpack, out_shape=(jax.ShapeDtypeStruct((width,), single),...  0.57 us

profile of v5, /device:TPU:0, one launch (start us, length us, event | category | flops | bytes accessed | tf_op | source)
XLA Modules:
  0.0 26.8 jit_solution(15963393902786413662)
XLA Ops:
  0.6 0.0 copy-start.3
  0.6 0.0 copy-start.1
  0.7 0.0 copy-start.2
  0.7 0.0 copy-start
  0.7 0.6 %copy-done.3 = f32[256]{0:T(256)S(1)} copy-done((f32[256]{0:T(256)S(1)}, f32[256]{0:T(256)}, u32[]{:S(2)}) %copy-start.3) | copy-done | bytes 1048
  1.3 0.0 copy-done.1
  1.3 0.0 copy-done.2
  1.3 0.0 copy-done
  1.4 24.8 %shard_map.103.packed_ref = f32[3,256]{1,0:T(4,128)S(1)} custom-call(f32[1,256]{1,0:T(1,128)S(1)} %bitcast.3, f32[1,256]{1,0:T(1,128)S(1)} %bitcast.4, f32[256,256]{1,0:T(8,128)} %self_ref.1, f32[256,256]{1,0:T(8,128)} %coup_ref.1, s32[2,2]{1,0:T(2,128)S(1)} %copy-done.2, f32[256,128]{1,0:T(8,128)} %pro_ref.1, f32[256,256]{1,0:T(8,128)} %craw_ref.1, ...), custom_call_target="tpu_custom_call" | custom-call | tf_op jit(solution)/shard_map/pallas_call | solution.py:719
  26.2 0.6 %shard_map.104 = (f32[256]{0:T(256)}, f32[256]{0:T(256)}, f32[3]{0:T(128)}) custom-call(f32[3,256]{1,0:T(4,128)S(1)} %shard_map.103.packed_ref), custom_call_target="tpu_custom_call" | custom-call | tf_op jit(solution)/shard_map/pallas_call | solution.py:760
Async XLA Ops:
  0.6 0.7 %copy-start.3 = (f32[256]{0:T(256)S(1)}, f32[256]{0:T(256)}, u32[]{:S(2)}) copy-start(f32[256]{0:T(256)} %param.15) | copy-start | bytes 3076
  0.6 0.7 %copy-start.1 = (f32[256]{0:T(256)S(1)}, f32[256]{0:T(256)}, u32[]{:S(2)}) copy-start(f32[256]{0:T(256)} %param.9) | copy-start | bytes 3076
  0.7 0.7 %copy-start.2 = (s32[2,2]{1,0:T(2,128)S(1)}, s32[2,2]{1,0:T(2,128)}, u32[]{:S(2)}) copy-start(s32[2,2]{1,0:T(2,128)} %pat_ref.1) | copy-start | bytes 52
  0.7 0.7 %copy-start = (f32[256]{0:T(256)S(1)}, f32[256]{0:T(256)}, u32[]{:S(2)}) copy-start(f32[256]{0:T(256)} %param.8) | copy-start | bytes 3076

commit v6 on v5

--- a/solution.py
+++ b/solution.py
@@ -124,10 +124,7 @@
     far = dom % 2
     near = 1 - far
     beyond = dom + 2 * far - 1
-    relays = n_col % 2 == 0
-    wide = jnp.logical_or(
-        jnp.logical_and(has_prev, dom % n_col == 0), jnp.logical_and(has_next, dom % n_col == n_col - 1)
-    )
+    wide = jnp.logical_or(jnp.logical_and(far == 0, has_prev), jnp.logical_and(far == 1, has_next))
     lane = lax.broadcasted_iota(jnp.int32, (1, LANES), 1)
 
     def remote(source, target, send, recv, device):
@@ -185,27 +182,25 @@
         line_copy().start()
         for index in range(3):
             mat_copy(index).start()
-        if relays:
-            @pl.when(wide)
+        @pl.when(wide)
+        def _():
+            pl.semaphore_wait(go, 1)
+
+            @pl.when(far == 0)
             def _():
-                pl.semaphore_wait(go, 1)
-
-                @pl.when(far == 0)
-                def _():
-                    halo_copy(self_ref).start()
-
-                @pl.when(far == 1)
-                def _():
-                    stage_copy().wait_recv()
-                    halo_copy(halo_mat).start()
+                halo_copy(self_ref).start()
+
+            @pl.when(far == 1)
+            def _():
+                stage_copy().wait_recv()
+                halo_copy(halo_mat).start()
 
         line_copy().wait_send()
         for index in range(3):
             mat_copy(index).wait_send()
-        if relays:
-            @pl.when(wide)
-            def _():
-                halo_copy(halo_mat).wait_send()
+        @pl.when(wide)
+        def _():
+            halo_copy(halo_mat).wait_send()
 
         pack_copy().wait_recv()
         sol, resid, uvec, wvec, pvec, svec = [pack_in[index : index + 1] for index in range(6)]
@@ -219,15 +214,16 @@
     @pl.when(sub == 1)
     def _():
         row_at, col_at = dom // n_col, dom % n_col
+        has_near = jnp.where(near == 1, has_next, has_prev)
+        has_far = jnp.where(near == 1, has_prev, has_next)
+        order = ((near, has_near), (far, has_far))
+
+        for side, exists in order[::-1]:
+            @pl.when(exists)
+            def _():
+                pl.semaphore_signal(barrier, inc=1, device_id=(dom + 2 * side - 1, 1), device_id_type=MESH)
+
         pl.semaphore_signal(barrier, inc=1, device_id=(dom, 0), device_id_type=MESH)
-
-        @pl.when(has_prev)
-        def _():
-            pl.semaphore_signal(barrier, inc=1, device_id=(dom - 1, 1), device_id_type=MESH)
-
-        @pl.when(has_next)
-        def _():
-            pl.semaphore_signal(barrier, inc=1, device_id=(dom + 1, 1), device_id_type=MESH)
 
         def in_row(step):
             return (row_at * n_col + (col_at + step) % n_col, 1)
@@ -258,13 +254,13 @@
             low_in[...] = jnp.zeros_like(low_in)
             edge_mat[0] = jnp.zeros_like(ft_mat)
             for k in range(1, 3 * ITERS):
-                in_buf[k, 0] = jnp.zeros((1, width), jnp.float32)
+                in_buf[0, k] = jnp.zeros((1, width), jnp.float32)
 
         @pl.when(dom == n_dom - 1)
         def _():
             up_in[...] = jnp.zeros_like(up_in)
             for k in range(1, 3 * ITERS):
-                in_buf[k, 1] = jnp.zeros((1, width), jnp.float32)
+                in_buf[1, k] = jnp.zeros((1, width), jnp.float32)
 
         def first_up():
             return remote(up_out, up_in, edge_send.at[0], edge_recv.at[0], (dom - 1, 1))
@@ -275,31 +271,27 @@
         def edge_matrix():
             return remote(ft_mat, edge_mat.at[0], edge_send.at[2], edge_recv.at[2], (dom + 1, 1))
 
-        def to_side(k, side, place=None):
-            source = out_buf.at[k if place is None else place, side]
-            return remote(
-                source, in_buf.at[k, 1 - side], out_send.at[k, side], in_recv.at[k, 1 - side], (dom + 2 * side - 1, 1)
-            )
-
-        def send(k, vec, wanted=(has_prev, has_next)):
-            for side in range(2):
-                out_buf[k, side] = vec[:, side * width : (side + 1) * width]
-
-                @pl.when(wanted[side])
+        def to_side(k, side, count=1, place=None):
+            source = out_buf.at[side, pl.ds(k if place is None else place, count)]
+            target = in_buf.at[1 - side, pl.ds(k, count)]
+            return remote(source, target, out_send.at[side, k], in_recv.at[1 - side, k], (dom + 2 * side - 1, 1))
+
+        def send(k, vecs, ways):
+            for index, vec in enumerate(vecs):
+                for side in range(2):
+                    out_buf[side, k + index] = vec[:, side * width : (side + 1) * width]
+            for side, exists in ways:
+                @pl.when(exists)
                 def _():
-                    to_side(k, side).start()
-
-        has_near = jnp.where(near == 1, has_next, has_prev)
-        has_far = jnp.where(near == 1, has_prev, has_next)
-        order = ((near, has_near), (far, has_far))
-
-        def receive(k, side, exists):
+                    to_side(k, side, len(vecs)).start()
+
+        def receive(k, side, exists, count=1):
             @pl.when(exists)
             def _():
-                landed = in_buf.at[k, side]
-                pltpu.make_async_copy(landed, landed, in_recv.at[k, side]).wait()
-
-            return in_buf[k, side]
+                landed = in_buf.at[side, pl.ds(k, count)]
+                pltpu.make_async_copy(landed, landed, in_recv.at[side, k]).wait()
+
+            return [in_buf[side, k + index] for index in range(count)]
 
         loads[0].wait()
         for i in range(blocks):
@@ -353,14 +345,13 @@
 
         for load in loads[1:]:
             load.wait()
-        if relays:
-            @pl.when(jnp.logical_and(wide, far == 1))
-            def _():
-                stage_copy().start()
-
-            @pl.when(jnp.logical_not(wide))
-            def _():
-                halo_mat[...] = jnp.zeros_like(halo_mat)
+        @pl.when(jnp.logical_and(wide, far == 1))
+        def _():
+            stage_copy().start()
+
+        @pl.when(jnp.logical_not(wide))
+        def _():
+            halo_mat[...] = jnp.zeros_like(halo_mat)
 
         put_self(1, diag_b)
         pt_mat[1] = p_raw[1].T
@@ -454,7 +445,7 @@
         def coarse_later(k, first, halo):
             base = fold(kt_mat[...], first)
             for side, exists in order:
-                row = receive(k, side, exists)
+                row, = receive(k, side, exists)
                 if halo is not None and side is far:
                     row = jnp.where(wide, halo[0] - halo[1] * row, row)
                 base = base + fold(ke_mat[side], row)
@@ -475,12 +466,8 @@
         def round_of(t, vec, begin, held=None):
             first = scale * vec
             halo = None
-            if held is not None:
-                send(3 * t, first, (
-                    jnp.logical_and(has_prev, dom % n_col != 0), jnp.logical_and(has_next, dom % n_col != n_col - 1)
-                ))
-            elif t:
-                send(3 * t, first)
+            if t:
+                send(3 * t, [first], order[::-1] if held is None else order[:1])
             begin()
             if held is not None:
                 column, lost = held
@@ -493,7 +480,7 @@
                 far_diag = OMEGA / far_scale
                 bare = jnp.where(same, 0.0, halo_mat[...])
                 strong = 0.5 * (flat(lanes(fold(bare, lost))) + down(bare, upright(lost))) + far_diag * lost
-                halo = in_buf[3, far] - far_scale * (down(edge_mat[far], column) - strong), far_scale
+                halo = in_buf[far, 3] - far_scale * (down(edge_mat[far], column) - strong), far_scale
             if t == 1:
                 edge_product(0)
             if t:
@@ -506,15 +493,16 @@
             second = first + jnp.concatenate(
                 [down(pt_mat[0], etwo[:coarse]), down(pt_mat[1], etwo[coarse:])], axis=1
             )
-            send(3 * t + 1, second)
             if t:
                 ghost = -scale * (turned + down(q_mat[...], etwo))
-                send(3 * t + 2, ghost)
+                send(3 * t + 1, [second, ghost], order[::-1])
+            else:
+                send(3 * t + 1, [second], order[::-1])
             base = {}
             for side, exists in order[::-1]:
                 base[side is far] = short(side, vec, second)
                 if not t:
-                    out_buf[2, side] = -side_of(side, scale) * flat(lanes(base[side is far]))
+                    out_buf[side, 2] = -side_of(side, scale) * flat(lanes(base[side is far]))
 
                     @pl.when(exists)
                     def _():
@@ -533,10 +521,9 @@
                 def _(step):
                     pl.semaphore_signal(known, inc=1, device_id=in_col(step), device_id_type=MESH)
 
-                if relays:
-                    @pl.when(wide)
-                    def _():
-                        pl.semaphore_signal(go, inc=1, device_id=(dom, 0), device_id_type=MESH)
+                @pl.when(wide)
+                def _():
+                    pl.semaphore_signal(go, inc=1, device_id=(dom, 0), device_id_type=MESH)
 
                 for side in range(2):
                     q_mat[side * coarse : (side + 1) * coarse] = product(pt_mat[side], t_mat[side])
@@ -545,7 +532,7 @@
             else:
                 for side in range(2):
                     side_buf[side] = rim_buf[side] * down(edge_mat[side], upper[side * width : (side + 1) * width])
-            early = relays and t == 1
+            early = t == 1
             if early:
                 blank = jnp.zeros((1, width), jnp.float32)
                 alone = jnp.concatenate(
@@ -559,33 +546,33 @@
                     def _():
                         edge_matrix().wait_recv()
 
-                ahead = receive(3 * t + 1, side, exists)
-                joint = t and not (early and side is near)
-                if joint:
-                    other = receive(3 * t + 2, side, exists) - side_buf[side]
+                if t:
+                    ahead, other = receive(3 * t + 1, side, exists, 2)
+                    other = other - side_buf[side]
+                else:
+                    ahead, = receive(3 * t + 1, side, exists)
                 total = base[side is far] + fold(edge_mat[side], ahead)
                 column = jnp.where(side == 0, minus[:width], minus[width:]) * lanes(total)
                 part = down(t_mat[side], column)
                 if early and side is near:
                     @pl.when(wide)
                     def _():
-                        out_buf[3 * ITERS, far] = side_of(far, part) + mine
-                        to_side(3 * t + 3, far, 3 * ITERS).start()
+                        out_buf[far, 3 * ITERS] = side_of(far, part) + mine
+                        to_side(3 * t + 3, far, 1, 3 * ITERS).start()
 
                 own = part if own is None else own + part
                 turned = flat(column)
                 if not t:
                     inner = jnp.where(side == 0, upper[:width], upper[width:])
                     lost = rim_buf[side] * down(edge_mat[side], inner)
-                    other = receive(3 * t + 2, side, exists) - lost
-                elif not joint:
-                    other = receive(3 * t + 2, side, exists) - side_buf[side]
+                    other = receive(3 * t + 2, side, exists)[0] - lost
                 crossed = flat(lanes(fold(edge_mat[side], other)))
                 mid_buf[side] = turned
                 end_buf[side] = crossed
             mvec = join(mid_buf)
             return mvec, own + heavy * mvec + join(end_buf), (column, side_buf[far]) if early else None
 
+        sent_slots = [(1, 1), (2, 1)] + [(3 * t + part, 1 + part) for t in range(1, ITERS) for part in range(2)]
         dvecs, yvecs, held = [rhs], [], None
         eta, cross = [], {}
 
@@ -664,22 +651,21 @@
         pack_out[6:7, :LANES] = misc
         pack_copy().start()
         pack_copy().wait_send()
-        if relays:
-            @pl.when(jnp.logical_and(wide, far == 1))
-            def _():
-                stage_copy().wait_send()
+        @pl.when(jnp.logical_and(wide, far == 1))
+        def _():
+            stage_copy().wait_send()
 
         @pl.when(has_prev)
         def _():
             first_up().wait_send()
-            for k in range(1, 3 * ITERS):
-                to_side(k, 0).wait_send()
+            for k, count in sent_slots:
+                to_side(k, 0, count).wait_send()
 
         @pl.when(has_next)
         def _():
             first_low().wait_send()
-            for k in range(1, 3 * ITERS):
-                to_side(k, 1).wait_send()
+            for k, count in sent_slots:
+                to_side(k, 1, count).wait_send()
 
         beta, alpha = finish(end_sums(last_sums), *final)
         put(
@@ -736,8 +722,8 @@
                 pltpu.VMEM((2 * coarse, 2 * width), single),
                 pltpu.VMEM((2, 2 * coarse, width), single),
                 pair, pair, pair, pair,
-                pltpu.VMEM((steps + 1, 2, 1, width), single),
-                pltpu.VMEM((steps, 2, 1, width), single),
+                pltpu.VMEM((2, steps + 1, 1, width), single),
+                pltpu.VMEM((2, steps, 1, width), single),
                 pair, pair, pair, pair,
                 pltpu.VMEM((2, 1, coarse), single),
                 pltpu.VMEM((2, 1, LANES), single),
@@ -747,7 +733,7 @@
                 square,
                 pltpu.SemaphoreType.REGULAR, pltpu.SemaphoreType.REGULAR, pltpu.SemaphoreType.REGULAR,
                 dma((4,)), dma, dma, dma((3,)), dma((3,)), dma((3,)), dma((3,)),
-                dma((steps, 2)), dma((steps, 2)),
+                dma((2, steps)), dma((2, steps)),
                 dma((2,)), dma((2,)), dma, dma, dma, dma, dma, dma,
             ],
             compiler_params=pltpu.CompilerParams(

time: 27 us -> 26.9 us (level)
  no operation moved by 1% of the time
where the time goes in v6:
time: 26.9 us; the launch traced here: 26.7 us
  Pallas kernels  25.3 us (94%)
  local copies, waits for them, and re-layouts  0.69 us (3%)
  between operations  0.67 us (2%)
    pallas_call x1, Pallas kernels, per_device(): pl.pallas_call(functools.partial(kernel, n_dom, n_sub), out_shape=jax.Sha...  24.8 us
    unnamed x8, local copies, waits for them, and re-layouts  0.69 us
    pallas_call x1, Pallas kernels, per_device(): pl.pallas_call(unpack, out_shape=(jax.ShapeDtypeStruct((width,), single),...  0.57 us

profile of v6, /device:TPU:0, one launch (start us, length us, event | category | flops | bytes accessed | tf_op | source)
XLA Modules:
  0.0 26.7 jit_solution(10348089764188876819)
XLA Ops:
  0.6 0.0 copy-start.3
  0.6 0.0 copy-start.1
  0.7 0.0 copy-start.2
  0.7 0.0 copy-start
  0.7 0.6 %copy-done.3 = f32[256]{0:T(256)S(1)} copy-done((f32[256]{0:T(256)S(1)}, f32[256]{0:T(256)}, u32[]{:S(2)}) %copy-start.3) | copy-done | bytes 1048
  1.3 0.0 copy-done.1
  1.3 0.0 copy-done.2
  1.3 0.0 copy-done
  1.4 24.8 %shard_map.103.packed_ref = f32[3,256]{1,0:T(4,128)S(1)} custom-call(f32[1,256]{1,0:T(1,128)S(1)} %bitcast.3, f32[1,256]{1,0:T(1,128)S(1)} %bitcast.4, f32[256,256]{1,0:T(8,128)} %self_ref.1, f32[256,256]{1,0:T(8,128)} %coup_ref.1, s32[2,2]{1,0:T(2,128)S(1)} %copy-done.2, f32[256,128]{1,0:T(8,128)} %pro_ref.1, f32[256,256]{1,0:T(8,128)} %craw_ref.1, ...), custom_call_target="tpu_custom_call" | custom-call | tf_op jit(solution)/shard_map/pallas_call | solution.py:705
  26.1 0.6 %shard_map.104 = (f32[256]{0:T(256)}, f32[256]{0:T(256)}, f32[3]{0:T(128)}) custom-call(f32[3,256]{1,0:T(4,128)S(1)} %shard_map.103.packed_ref), custom_call_target="tpu_custom_call" | custom-call | tf_op jit(solution)/shard_map/pallas_call | solution.py:746
Async XLA Ops:
  0.6 0.7 %copy-start.3 = (f32[256]{0:T(256)S(1)}, f32[256]{0:T(256)}, u32[]{:S(2)}) copy-start(f32[256]{0:T(256)} %param.15) | copy-start | bytes 3076
  0.6 0.7 %copy-start.1 = (f32[256]{0:T(256)S(1)}, f32[256]{0:T(256)}, u32[]{:S(2)}) copy-start(f32[256]{0:T(256)} %param.9) | copy-start | bytes 3076
  0.7 0.7 %copy-start.2 = (s32[2,2]{1,0:T(2,128)S(1)}, s32[2,2]{1,0:T(2,128)}, u32[]{:S(2)}) copy-start(s32[2,2]{1,0:T(2,128)} %pat_ref.1) | copy-start | bytes 52
  0.7 0.7 %copy-start = (f32[256]{0:T(256)S(1)}, f32[256]{0:T(256)}, u32[]{:S(2)}) copy-start(f32[256]{0:T(256)} %param.8) | copy-start | bytes 3076

commit v7 on v6

--- a/solution.py
+++ b/solution.py
@@ -107,7 +107,7 @@
     lines, s_raw, c_raw, p_raw, k_raw,
     edge_mat, ft_mat, t_mat, pt_mat, k_mat, q_mat, kt_mat, ke_mat,
     up_out, low_out, up_in, low_in, out_buf, in_buf, rim_buf, side_buf, mid_buf, end_buf, rough_buf,
-    part_buf, red_buf, pack_out, pack_in, halo_mat,
+    part_buf, red_buf, tail_buf, wide_buf, pack_out, pack_in, halo_mat,
     met, known, go, load_sem, line_send, line_recv, mat_send, mat_recv, edge_send, edge_recv,
     out_send, in_recv, r_send, r_recv, pack_send, pack_recv, halo_send, halo_recv, stage_send, stage_recv,
 ):
@@ -153,7 +153,7 @@
         return remote(source, halo_mat, halo_send, halo_recv, (beyond, 1))
 
     def finish(sums, known_gamma, gamma_at, known_delta, delta_at, delta_next, gamma_inv, alpha_inv):
-        even, odd = pick(sums, 0), pick(sums, 1)
+        even, odd = lanes(sums[0]), lanes(sums[1])
         gamma = known_gamma + gamma_at * even
         delta = known_delta + delta_at * even + delta_next * odd
         beta = gamma * gamma_inv
@@ -206,9 +206,8 @@
         sol, resid, uvec, wvec, pvec, svec = [pack_in[index : index + 1] for index in range(6)]
         misc = pack_in[6:7]
         scalars = [pick(misc, place) for place in range(7 + ITERS)]
-        every = red_buf.at[last_sums]
-        pltpu.make_async_copy(every, every, r_recv.at[last_sums]).wait()
-        beta, alpha = finish(jnp.sum(red_buf[last_sums], axis=0), *scalars[:7])
+        pltpu.make_async_copy(wide_buf, wide_buf, r_recv.at[last_sums]).wait()
+        beta, alpha = finish(jnp.sum(wide_buf[...], axis=0), *scalars[:7])
         put(sol + alpha * (uvec + beta * pvec), resid - alpha * (wvec + beta * svec), scalars[7:])
 
     @pl.when(sub == 1)
@@ -378,33 +377,47 @@
         def dot(left, right):
             return lanes(left * right)
 
-        def start_sums(step, values):
+        def strip(row):
+            return sum(row[:, start : start + LANES] for start in range(0, row.shape[1], LANES))
+
+        def each_other(run):
+            @pl.loop(0, n_dom - 1)
+            def _(index):
+                run(index + (index >= dom).astype(jnp.int32))
+
+        def start_sums(values):
             line = jnp.zeros((1, LANES), jnp.float32)
             for place, value in enumerate(values):
                 line = jnp.where(lane == place, value, line)
-            part_buf[step] = line
-            red_buf[step, pl.ds(dom, 1)] = line[None]
-            if step == first_sums:
-                pl.semaphore_wait(known, n_row - 1)
-
-            @pl.loop(0, n_dom - 1)
-            def _(index):
-                target = index + (index >= dom).astype(jnp.int32)
-                for other in range(n_sub) if step == last_sums else (1,):
-                    remote(
-                        part_buf.at[step], red_buf.at[step, dom], r_send.at[step], r_recv.at[step],
-                        (target, other),
-                    ).start()
-
-            if step == last_sums:
-                remote(
-                    part_buf.at[step], red_buf.at[step, dom], r_send.at[step], r_recv.at[step], (dom, 0)
-                ).start()
+            part_buf[...] = line
+            red_buf[pl.ds(dom, 1)] = line[None]
+            pl.semaphore_wait(known, n_row - 1)
+            each_other(lambda target: remote(
+                part_buf, red_buf.at[dom], r_send.at[first_sums], r_recv.at[first_sums], (target, 1)
+            ).start())
+
+        def last_copy(target, other):
+            return remote(
+                tail_buf, wide_buf.at[dom], r_send.at[last_sums], r_recv.at[last_sums], (target, other)
+            )
+
+        def start_last(rows):
+            for index, row in enumerate(rows):
+                tail_buf[index] = strip(row)
+                wide_buf[dom, index] = strip(row)
+
+            def run(target):
+                for other in range(n_sub):
+                    last_copy(target, other).start()
+
+            each_other(run)
+            last_copy(dom, 0).start()
 
         def end_sums(step):
-            others = red_buf.at[step, pl.ds(0, n_dom - 1)]
+            buffer = (red_buf, wide_buf)[step]
+            others = buffer.at[pl.ds(0, n_dom - 1)]
             pltpu.make_async_copy(others, others, r_recv.at[step]).wait()
-            return jnp.sum(red_buf[step], axis=0)
+            return jnp.sum(buffer[...], axis=0)
 
         def join(buffer):
             return jnp.concatenate([buffer[0], buffer[1]], axis=1)
@@ -586,7 +599,7 @@
                 else:
                     cross[0, 0] = dot(rhs, rhs)
                 if t == last:
-                    start_sums(first_sums, eta + [cross[place] for place in sorted(cross)])
+                    start_sums(eta + [cross[place] for place in sorted(cross)])
 
             return begin
 
@@ -596,7 +609,7 @@
             dvecs.append(dvecs[t] - bvec)
             if t < last:
                 eta.append(dot(dvecs[t], yvec))
-        start_sums(last_sums, [dot(dvecs[last], yvecs[last]), dot(dvecs[ITERS], yvecs[last])])
+        start_last([dvecs[last] * yvecs[last], dvecs[ITERS] * yvecs[last]])
 
         sums = end_sums(first_sums)
         count = 2 * last
@@ -674,12 +687,10 @@
             norm_list,
         )
 
-        for step in (first_sums, last_sums):
-            sent = red_buf.at[step, pl.ds(0, n_dom - 1)]
+        for step, buffer in ((first_sums, red_buf), (last_sums, wide_buf)):
+            sent = buffer.at[pl.ds(0, n_dom - 1)]
             pltpu.make_async_copy(sent, sent, r_send.at[step]).wait()
-            if step == last_sums:
-                every = red_buf.at[step]
-                pltpu.make_async_copy(every, every, r_send.at[step]).wait()
+        pltpu.make_async_copy(wide_buf, wide_buf, r_send.at[last_sums]).wait()
 
 
 def unpack(packed_ref, sol_ref, res_ref, norm_ref):
@@ -726,8 +737,10 @@
                 pltpu.VMEM((2, steps, 1, width), single),
                 pair, pair, pair, pair,
                 pltpu.VMEM((2, 1, coarse), single),
+                pltpu.VMEM((1, LANES), single),
+                pltpu.VMEM((n_dom, 1, LANES), single),
                 pltpu.VMEM((2, 1, LANES), single),
-                pltpu.VMEM((2, n_dom, 1, LANES), single),
+                pltpu.VMEM((n_dom, 2, 1, LANES), single),
                 pltpu.VMEM((8, width), single),
                 pltpu.VMEM((8, width), single),
                 square,

time: 26.9 us -> 26.8 us (level)
  no operation moved by 1% of the time
where the time goes in v7:
time: 26.8 us; the launch traced here: 26.6 us
  Pallas kernels  25.3 us (94%)
  local copies, waits for them, and re-layouts  0.69 us (3%)
  between operations  0.67 us (2%)
    pallas_call x1, Pallas kernels, per_device(): pl.pallas_call(functools.partial(kernel, n_dom, n_sub), out_shape=jax.Sha...  24.7 us
    unnamed x8, local copies, waits for them, and re-layouts  0.69 us
    pallas_call x1, Pallas kernels, per_device(): pl.pallas_call(unpack, out_shape=(jax.ShapeDtypeStruct((width,), single),...  0.57 us

profile of v7, /device:TPU:0, one launch (start us, length us, event | category | flops | bytes accessed | tf_op | source)
XLA Modules:
  0.0 26.6 jit_solution(10469139930903685158)
XLA Ops:
  0.6 0.0 copy-start.3
  0.6 0.0 copy-start.1
  0.7 0.0 copy-start.2
  0.7 0.0 copy-start
  0.7 0.6 %copy-done.3 = f32[256]{0:T(256)S(1)} copy-done((f32[256]{0:T(256)S(1)}, f32[256]{0:T(256)}, u32[]{:S(2)}) %copy-start.3) | copy-done | bytes 1048
  1.3 0.0 copy-done.1
  1.3 0.0 copy-done.2
  1.3 0.0 copy-done
  1.4 24.7 %shard_map.103.packed_ref = f32[3,256]{1,0:T(4,128)S(1)} custom-call(f32[1,256]{1,0:T(1,128)S(1)} %bitcast.3, f32[1,256]{1,0:T(1,128)S(1)} %bitcast.4, f32[256,256]{1,0:T(8,128)} %self_ref.1, f32[256,256]{1,0:T(8,128)} %coup_ref.1, s32[2,2]{1,0:T(2,128)S(1)} %copy-done.2, f32[256,128]{1,0:T(8,128)} %pro_ref.1, f32[256,256]{1,0:T(8,128)} %craw_ref.1, ...), custom_call_target="tpu_custom_call" | custom-call | tf_op jit(solution)/shard_map/pallas_call | solution.py:716
  26.1 0.6 %shard_map.104 = (f32[256]{0:T(256)}, f32[256]{0:T(256)}, f32[3]{0:T(128)}) custom-call(f32[3,256]{1,0:T(4,128)S(1)} %shard_map.103.packed_ref), custom_call_target="tpu_custom_call" | custom-call | tf_op jit(solution)/shard_map/pallas_call | solution.py:759
Async XLA Ops:
  0.6 0.7 %copy-start.3 = (f32[256]{0:T(256)S(1)}, f32[256]{0:T(256)}, u32[]{:S(2)}) copy-start(f32[256]{0:T(256)} %param.15) | copy-start | bytes 3076
  0.6 0.7 %copy-start.1 = (f32[256]{0:T(256)S(1)}, f32[256]{0:T(256)}, u32[]{:S(2)}) copy-start(f32[256]{0:T(256)} %param.9) | copy-start | bytes 3076
  0.7 0.7 %copy-start.2 = (s32[2,2]{1,0:T(2,128)S(1)}, s32[2,2]{1,0:T(2,128)}, u32[]{:S(2)}) copy-start(s32[2,2]{1,0:T(2,128)} %pat_ref.1) | copy-start | bytes 52
  0.7 0.7 %copy-start = (f32[256]{0:T(256)S(1)}, f32[256]{0:T(256)}, u32[]{:S(2)}) copy-start(f32[256]{0:T(256)} %param.8) | copy-start | bytes 3076
